TPU v7x, 128 devices: a whole 4x4x4 slice. The times are simulated.
128 devices in a mesh: dp: 32 (over y, x, core), leaf: 4 (over z).
Axes of the slice: x: 4, y: 4, z: 4, core: 2. Of those that a mesh axis runs over, the one named last changes fastest.
Arguments:
- predict: float32 [100, 1048576], P(None, ('dp', 'leaf')), may hold values from -6 to 256
- labels: int32 [1048576], P(('dp', 'leaf')), may hold values from 0 to 99
- leaf_ids: int32 [32, 1048576], P(None, ('dp', 'leaf')), may hold values from 0 to 63
Outputs:
- new_predict: float32 [100, 1048576], P(None, ('dp', 'leaf'))
- leaf_values: float32 [100, 2048], P(None, 'leaf')
All inputs are finite; a program needn't handle non-finite values.
Results may differ from a plain program's by a relative error of at most 0.0044.
Values sent between devices are 32-bit elements; how exact they have to be, the bound alone decides.
A program may use at most 64 MiB of HBM per device.

v0:
```python
import jax
import jax.numpy as jnp
from jax import lax
from jax.sharding import Mesh
from jax.sharding import PartitionSpec as P

LEAVES = 64
DP_LEAF = ("dp_0", "dp_1", "dp_2", "leaf")


step_size = 0.5
ridge_term = 1.0


def in_blocks(shard, dim, length):
    before, after = (shard.shape[:dim], shard.shape[dim + 1 :])
    return jnp.moveaxis(shard.reshape(*before, length, -1, *after), dim, 0)


def sent_and_summed(shard, axis, dim):
    length = lax.axis_size(axis)
    blocks = lax.all_to_all(in_blocks(shard, dim, length), axis, 0, 0, tiled=True)
    return jnp.sum(blocks, axis=0)


def sum_by_axis(shard, axes, dim):
    far, near = axes
    blocks = in_blocks(shard, dim, lax.axis_size(far))
    nearer = sent_and_summed(blocks, near, dim + 1)
    arrived = lax.all_to_all(nearer, far, split_axis=0, concat_axis=0, tiled=True)
    return arrived.sum(axis=0)


def rows_for(lines, length):
    spare = -len(lines) % length
    return jnp.pad(lines, [(0, spare)] + [(0, 0)] * (lines.ndim - 1))


def from_everyone(shard, axis):
    length = lax.axis_size(axis)
    return lax.all_to_all(
        jnp.broadcast_to(shard[None], (length, *shard.shape)), axis, 0, 0, tiled=True
    )


def joined_along(blocks, dim):
    blocks = jnp.moveaxis(blocks, 0, dim)
    dims = blocks.shape
    return blocks.reshape(*dims[:dim], dims[dim] * dims[dim + 1], *dims[dim + 2 :])


def whole_of(shard, axes, dim):
    far, near = axes
    leading = from_everyone(shard, far)
    blocks = jnp.swapaxes(from_everyone(leading, near), 0, 1)
    return joined_along(blocks.reshape(-1, *shard.shape), dim)


def nested_sum(shard, axes):
    lines = shard.reshape(-1)
    own = sum_by_axis(rows_for(lines, lax.axis_size(axes[0]) * lax.axis_size(axes[1])), axes, 0)
    whole = whole_of(own, axes, 0)
    return whole[: len(lines)].reshape(shard.shape)


def gradients(predict, labels):
    row_max = jnp.max(predict, axis=0, keepdims=True)
    exponent = jnp.exp(predict - row_max)
    probability = exponent / jnp.sum(exponent, axis=0, keepdims=True)
    classes = lax.broadcasted_iota(jnp.int32, predict.shape, 0)
    targets = (classes == labels[None, :]).astype(jnp.float32)
    gradient = (probability - targets).astype(jnp.bfloat16)
    hessian = (probability * (1.0 - probability)).astype(jnp.bfloat16)
    return jnp.concatenate([gradient, hessian], axis=0)


def block_rows(row_count):
    return min(row_count, 1024)


def leaf_table(tree_ids, first_row, width):
    id_block = lax.dynamic_slice_in_dim(tree_ids, first_row, width, 1)
    leaf_slot = lax.broadcasted_iota(jnp.int32, (id_block.shape[0], LEAVES, width), 1)
    matches = id_block[:, None, :] == leaf_slot
    return matches.astype(jnp.bfloat16).reshape(id_block.shape[0] * LEAVES, width)


def local_sums(stacked, leaf_ids):
    row_count = stacked.shape[1]
    width = block_rows(row_count)
    initial = jnp.zeros((stacked.shape[0], leaf_ids.shape[0] * LEAVES), jnp.float32)

    def local_advance(counter, running):
        first_row = counter * width
        partial_value = lax.dynamic_slice_in_dim(stacked, first_row, width, 1)
        one_hot = leaf_table(leaf_ids, first_row, width)
        return running + lax.dot_general(
            partial_value, one_hot, (((1,), (1,)), ((), ())), preferred_element_type=jnp.float32
        )

    return lax.fori_loop(0, row_count // width, local_advance, initial)


def newton(totals):
    classes = totals.shape[0] // 2
    return -step_size * totals[:classes] / (totals[classes:] + ridge_term)


def apply_values(carried, values, tree_ids):
    row_count = tree_ids.shape[1]
    width = block_rows(row_count)
    high_part = values.astype(jnp.bfloat16)
    low_part = (values - high_part.astype(jnp.float32)).astype(jnp.bfloat16)

    def apply_advance(counter, running):
        first_row = counter * width
        one_hot = leaf_table(tree_ids, first_row, width)
        partial_value = jnp.dot(high_part, one_hot, preferred_element_type=jnp.float32)
        partial_value = partial_value + jnp.dot(
            low_part, one_hot, preferred_element_type=jnp.float32
        )
        previous = lax.dynamic_slice_in_dim(running, first_row, width, 1)
        return lax.dynamic_update_slice_in_dim(running, previous + partial_value, first_row, 1)

    return lax.fori_loop(0, row_count // width, apply_advance, carried)


def shards(predict, labels, leaf_ids):
    stacked = gradients(predict, labels)
    leaf_sums = local_sums(stacked, leaf_ids)
    own_width = leaf_ids.shape[0] * LEAVES // lax.axis_size("leaf")
    initial = jnp.zeros(predict.shape, jnp.float32)
    totals = nested_sum(leaf_sums, (("dp_0", "dp_1"), ("dp_2", "leaf")))
    all_values = newton(totals)
    own_values = lax.dynamic_slice_in_dim(
        all_values, lax.axis_index("leaf") * own_width, own_width, 1
    )
    update = apply_values(initial, all_values, leaf_ids)
    return (predict + update, own_values)


def solution(mesh):
    finer = Mesh(
        mesh.devices.reshape(4, 4, 2, mesh.shape["leaf"]), ("dp_0", "dp_1", "dp_2", "leaf")
    )
    in_specs = (P(None, DP_LEAF), P(DP_LEAF), P(None, DP_LEAF))
    out_specs = (P(None, DP_LEAF), P(None, "leaf"))
    return jax.shard_map(
        shards, mesh=finer, in_specs=in_specs, out_specs=out_specs, check_vma=False
    )
```

profile of v0, /device:TPU:1, one launch (start us, length us, event | category | flops | bytes accessed | tf_op | source)
XLA Modules:
  0.0 217.8 jit_solution(10719852692999979483)
XLA Ops:
  0.7 2.3 %reduce_max.9 = f32[8192]{0:T(1024)S(1)} reduce(f32[100,8192]{1,0:T(8,128)} %param.7, f32[]{:T(128)} %constant.71.clone.1), dimensions={0}, to_apply=%region_0.0 | reduce | flops 811008 | bytes 3309572 | tf_op jit(solution)/shard_map/reduce_max | solution.py:67
  5.6 2.2 %pad_maximum_fusion = bf16[200,8192]{1,0:T(8,128)(2,1)} fusion(bf16[100,8192]{1,0:T(8,128)(2,1)S(1)} %get-tuple-element.213, bf16[100,8192]{1,0:T(8,128)(2,1)S(1)} %get-tuple-element.212), kind=kLoop, calls=%fused_computation.16 | loop fusion | flops 6553600 | bytes 6553600 | tf_op jit(solution)/shard_map/concatenate | solution.py:74
  7.9 51.1 %while.28 = (s32[]{:T(128)}, f32[200,2048]{1,0:T(8,128)}, bf16[200,8192]{1,0:T(8,128)(2,1)}, s32[32,8192]{1,0:T(8,128)}, s32[]{:T(128)}, /*index=5*/s32[]{:T(128)}, s32[]{:T(128)}, s32[]{:T(128)}) while((s32[]{:T(128)}, f32[200,2048]{1,0:T(8,128)}, bf16[200,8192]{1,0:T(8,128)(2,1)}, s32[32,8192]{1,0:T(8,128)}, s32[]{:T(128)}, ...), condition=%wide.region_3.0_spmd.clone, body=%wide.region_2.0_spmd.clone.sunk | while | flops 841777152 | bytes 21414100 | solution.py:101
  9.0 1.3 bitcast_compare_fusion.5
  10.3 2.7 %convolution_add_fusion.3 = f32[200,2048]{1,0:T(8,128)S(1)} fusion(pred[2048,1024]{1,0:T(32,128)(4,1)S(1)} %bitcast_compare_fusion.5, f32[200,2048]{1,0:T(8,128)S(1)} %copy-done.1, pred[]{:T(512)S(6)} %compare.3, bf16[200,8192]{1,0:T(8,128)(2,1)} %get-tuple-element.288, s32[]{:T(128)S(6)} %select_n.25), kind=kOutput, calls=%fused_computation.7.clone.1 | convolution fusion | flops 839680000 | bytes 5783557 | tf_op jit(solution)/shard_map/while/body/eval_jaxpr/dot_general | solution.py:97
  15.4 1.3 bitcast_compare_fusion.5
  16.7 2.7 %convolution_add_fusion.3 = f32[200,2048]{1,0:T(8,128)S(1)} fusion(pred[2048,1024]{1,0:T(32,128)(4,1)S(1)} %bitcast_compare_fusion.5, f32[200,2048]{1,0:T(8,128)S(1)} %copy-done.1, pred[]{:T(512)S(6)} %compare.3, bf16[200,8192]{1,0:T(8,128)(2,1)} %get-tuple-element.288, s32[]{:T(128)S(6)} %select_n.25), kind=kOutput, calls=%fused_computation.7.clone.1 | convolution fusion | flops 839680000 | bytes 5783557 | tf_op jit(solution)/shard_map/while/body/eval_jaxpr/dot_general | solution.py:97
  21.8 1.3 bitcast_compare_fusion.5
  23.1 2.7 %convolution_add_fusion.3 = f32[200,2048]{1,0:T(8,128)S(1)} fusion(pred[2048,1024]{1,0:T(32,128)(4,1)S(1)} %bitcast_compare_fusion.5, f32[200,2048]{1,0:T(8,128)S(1)} %copy-done.1, pred[]{:T(512)S(6)} %compare.3, bf16[200,8192]{1,0:T(8,128)(2,1)} %get-tuple-element.288, s32[]{:T(128)S(6)} %select_n.25), kind=kOutput, calls=%fused_computation.7.clone.1 | convolution fusion | flops 839680000 | bytes 5783557 | tf_op jit(solution)/shard_map/while/body/eval_jaxpr/dot_general | solution.py:97
  28.1 1.3 bitcast_compare_fusion.5
  29.5 2.7 %convolution_add_fusion.3 = f32[200,2048]{1,0:T(8,128)S(1)} fusion(pred[2048,1024]{1,0:T(32,128)(4,1)S(1)} %bitcast_compare_fusion.5, f32[200,2048]{1,0:T(8,128)S(1)} %copy-done.1, pred[]{:T(512)S(6)} %compare.3, bf16[200,8192]{1,0:T(8,128)(2,1)} %get-tuple-element.288, s32[]{:T(128)S(6)} %select_n.25), kind=kOutput, calls=%fused_computation.7.clone.1 | convolution fusion | flops 839680000 | bytes 5783557 | tf_op jit(solution)/shard_map/while/body/eval_jaxpr/dot_general | solution.py:97
  34.5 1.3 bitcast_compare_fusion.5
  35.9 2.7 %convolution_add_fusion.3 = f32[200,2048]{1,0:T(8,128)S(1)} fusion(pred[2048,1024]{1,0:T(32,128)(4,1)S(1)} %bitcast_compare_fusion.5, f32[200,2048]{1,0:T(8,128)S(1)} %copy-done.1, pred[]{:T(512)S(6)} %compare.3, bf16[200,8192]{1,0:T(8,128)(2,1)} %get-tuple-element.288, s32[]{:T(128)S(6)} %select_n.25), kind=kOutput, calls=%fused_computation.7.clone.1 | convolution fusion | flops 839680000 | bytes 5783557 | tf_op jit(solution)/shard_map/while/body/eval_jaxpr/dot_general | solution.py:97
  40.9 1.3 bitcast_compare_fusion.5
  42.3 2.7 %convolution_add_fusion.3 = f32[200,2048]{1,0:T(8,128)S(1)} fusion(pred[2048,1024]{1,0:T(32,128)(4,1)S(1)} %bitcast_compare_fusion.5, f32[200,2048]{1,0:T(8,128)S(1)} %copy-done.1, pred[]{:T(512)S(6)} %compare.3, bf16[200,8192]{1,0:T(8,128)(2,1)} %get-tuple-element.288, s32[]{:T(128)S(6)} %select_n.25), kind=kOutput, calls=%fused_computation.7.clone.1 | convolution fusion | flops 839680000 | bytes 5783557 | tf_op jit(solution)/shard_map/while/body/eval_jaxpr/dot_general | solution.py:97
  47.3 1.3 bitcast_compare_fusion.5
  48.7 2.7 %convolution_add_fusion.3 = f32[200,2048]{1,0:T(8,128)S(1)} fusion(pred[2048,1024]{1,0:T(32,128)(4,1)S(1)} %bitcast_compare_fusion.5, f32[200,2048]{1,0:T(8,128)S(1)} %copy-done.1, pred[]{:T(512)S(6)} %compare.3, bf16[200,8192]{1,0:T(8,128)(2,1)} %get-tuple-element.288, s32[]{:T(128)S(6)} %select_n.25), kind=kOutput, calls=%fused_computation.7.clone.1 | convolution fusion | flops 839680000 | bytes 5783557 | tf_op jit(solution)/shard_map/while/body/eval_jaxpr/dot_general | solution.py:97
  53.7 1.3 bitcast_compare_fusion.5
  55.1 2.7 %convolution_add_fusion.3 = f32[200,2048]{1,0:T(8,128)S(1)} fusion(pred[2048,1024]{1,0:T(32,128)(4,1)S(1)} %bitcast_compare_fusion.5, f32[200,2048]{1,0:T(8,128)S(1)} %copy-done.1, pred[]{:T(512)S(6)} %compare.3, bf16[200,8192]{1,0:T(8,128)(2,1)} %get-tuple-element.288, s32[]{:T(128)S(6)} %select_n.25), kind=kOutput, calls=%fused_computation.7.clone.1 | convolution fusion | flops 839680000 | bytes 5783557 | tf_op jit(solution)/shard_map/while/body/eval_jaxpr/dot_general | solution.py:97
  59.0 3.0 %reshape_reshape.3 = f32[16,8,3200]{2,1,0:T(8,128)} reshape(f32[200,2048]{1,0:T(8,128)} %get-tuple-element.175) | data formatting | bytes 3276800 | tf_op jit(solution)/shard_map/reshape;reshape | solution.py:17
  62.0 1.7 copy.5
  63.7 28.3 %all_to_all.25 = f32[8,16,3200]{2,1,0:T(8,128)} all-to-all(f32[8,16,3200]{2,1,0:T(8,128)S(1)} %copy.5), channel_id=1, replica_groups=mesh['dp_0'=4,'dp_1'=4,'dp_2'=2,'leaf'=4] {'dp_2','leaf'}, dimensions={0} | all-to-all | bytes 3276800 | tf_op jit(solution)/shard_map/all_to_all | solution.py:22
  92.1 2.2 %reduce_sum.28 = f32[16,3200]{1,0:T(8,128)} reduce(f32[8,16,3200]{2,1,0:T(8,128)} %all_to_all.25, f32[]{:T(128)} %constant.70.clone.1), dimensions={0}, to_apply=%region_4.5 | reduce | flops 358400 | bytes 1843204 | tf_op jit(solution)/shard_map/reduce_sum | solution.py:23
  95.3 13.9 %all_to_all.26 = f32[16,1,3200]{2,1,0:T(1,128)} all-to-all(f32[16,1,3200]{2,1,0:T(1,128)S(1)} %all_to_all.17), channel_id=1, replica_groups=mesh['dp_0'=4,'dp_1'=4,'dp_2'=2,'leaf'=4] {'dp_0','dp_1'}, dimensions={0} | all-to-all | bytes 409600 | tf_op jit(solution)/shard_map/all_to_all | solution.py:30
  110.4 10.2 %all_to_all.27 = f32[16,1,3200]{2,1,0:T(1,128)S(1)} all-to-all(f32[16,1,3200]{2,1,0:T(1,128)S(1)} %broadcast_in_dim.31), channel_id=1, replica_groups=mesh['dp_0'=4,'dp_1'=4,'dp_2'=2,'leaf'=4] {'dp_0','dp_1'}, dimensions={0} | all-to-all | bytes 409600 | tf_op jit(solution)/shard_map/all_to_all | solution.py:41
  121.9 7.2 %all-to-all-start.3 = ((f32[8,16,3200]{2,1,0:T(8,128)}), f32[8,16,3200]{2,1,0:T(8,128)}, u32[]{:S(2)}, u32[]{:S(2)}) async-start(f32[8,16,3200]{2,1,0:T(8,128)} %broadcast_in_dim.33), calls=%async_computation.3 | async-start | bytes 3276800 | tf_op jit(solution)/shard_map/all_to_all | solution.py:41
  129.1 21.4 %all-to-all-done.3 = f32[8,16,3200]{2,1,0:T(8,128)} async-done(((f32[8,16,3200]{2,1,0:T(8,128)}), f32[8,16,3200]{2,1,0:T(8,128)}, u32[]{:S(2)}, u32[]{:S(2)}) %all-to-all-start.3) | async-done | bytes 1638432 | tf_op jit(solution)/shard_map/all_to_all | solution.py:41
  150.5 1.5 fusion.8
  153.0 2.3 %div.17 = f32[100,2048]{1,0:T(8,128)} reshape(f32[8,8,3200]{2,1,0:T(8,128)} %copy.6) | data formatting | bytes 1638400 | tf_op jit(solution)/shard_map/div | solution.py:106
  155.3 2.4 %subtract_convert_fusion.1 = (bf16[100,2048]{1,0:T(8,128)(2,1)}, bf16[100,2048]{1,0:T(8,128)(2,1)}) fusion(f32[100,2048]{1,0:T(8,128)} %div.17), kind=kLoop, calls=%fused_computation.19 | loop fusion | flops 819200 | bytes 1638400 | tf_op jit(solution)/shard_map/convert_element_type | solution.py:113
  157.8 1.6 constant_dynamic-slice_fusion.2
  159.4 2.1 broadcast_in_dim.15
  161.5 52.3 %while.27 = (s32[]{:T(128)}, f32[100,8192]{1,0:T(8,128)}, s32[32,8192]{1,0:T(8,128)}, bf16[100,2048]{1,0:T(8,128)(2,1)}, bf16[100,2048]{1,0:T(8,128)(2,1)}, /*index=5*/s32[]{:T(128)}, s32[]{:T(128)}, s32[]{:T(128)}, s32[]{:T(128)}) while((s32[]{:T(128)}, f32[100,8192]{1,0:T(8,128)}, s32[32,8192]{1,0:T(8,128)}, bf16[100,2048]{1,0:T(8,128)(2,1)}, ...), condition=%wide.region_7.8_spmd, body=%wide.region_6.7_spmd.sunk | while | flops 841162752 | bytes 12484811 | solution.py:125
  165.1 2.9 %fusion.28 = f32[100,8192]{1,0:T(8,128)} fusion(f32[100,8192]{1,0:T(8,128)} %get-tuple-element.304, s32[]{:T(128)S(6)} %select_n.24, f32[1024,100]{0,1:T(8,128)S(1)} %fusion.27, pred[2048,1024]{1,0:T(32,128)(4,1)S(1)} %bitcast_compare_fusion.4, bf16[100,2048]{1,0:T(8,128)(2,1)S(1)} %copy-done.3), kind=kOutput, calls=%fused_computation.4.clone.1 | convolution fusion | flops 419635200 | bytes 3768324 | tf_op jit(solution)/shard_map/while/body/eval_jaxpr/dot_general | solution.py:119
  169.0 1.3 bitcast_compare_fusion.4
  171.6 2.9 %fusion.28 = f32[100,8192]{1,0:T(8,128)} fusion(f32[100,8192]{1,0:T(8,128)} %get-tuple-element.304, s32[]{:T(128)S(6)} %select_n.24, f32[1024,100]{0,1:T(8,128)S(1)} %fusion.27, pred[2048,1024]{1,0:T(32,128)(4,1)S(1)} %bitcast_compare_fusion.4, bf16[100,2048]{1,0:T(8,128)(2,1)S(1)} %copy-done.3), kind=kOutput, calls=%fused_computation.4.clone.1 | convolution fusion | flops 419635200 | bytes 3768324 | tf_op jit(solution)/shard_map/while/body/eval_jaxpr/dot_general | solution.py:119
  175.6 1.3 bitcast_compare_fusion.4
  178.1 2.9 %fusion.28 = f32[100,8192]{1,0:T(8,128)} fusion(f32[100,8192]{1,0:T(8,128)} %get-tuple-element.304, s32[]{:T(128)S(6)} %select_n.24, f32[1024,100]{0,1:T(8,128)S(1)} %fusion.27, pred[2048,1024]{1,0:T(32,128)(4,1)S(1)} %bitcast_compare_fusion.4, bf16[100,2048]{1,0:T(8,128)(2,1)S(1)} %copy-done.3), kind=kOutput, calls=%fused_computation.4.clone.1 | convolution fusion | flops 419635200 | bytes 3768324 | tf_op jit(solution)/shard_map/while/body/eval_jaxpr/dot_general | solution.py:119
  182.1 1.3 bitcast_compare_fusion.4
  184.7 2.9 %fusion.28 = f32[100,8192]{1,0:T(8,128)} fusion(f32[100,8192]{1,0:T(8,128)} %get-tuple-element.304, s32[]{:T(128)S(6)} %select_n.24, f32[1024,100]{0,1:T(8,128)S(1)} %fusion.27, pred[2048,1024]{1,0:T(32,128)(4,1)S(1)} %bitcast_compare_fusion.4, bf16[100,2048]{1,0:T(8,128)(2,1)S(1)} %copy-done.3), kind=kOutput, calls=%fused_computation.4.clone.1 | convolution fusion | flops 419635200 | bytes 3768324 | tf_op jit(solution)/shard_map/while/body/eval_jaxpr/dot_general | solution.py:119
  188.6 1.3 bitcast_compare_fusion.4
  191.2 2.9 %fusion.28 = f32[100,8192]{1,0:T(8,128)} fusion(f32[100,8192]{1,0:T(8,128)} %get-tuple-element.304, s32[]{:T(128)S(6)} %select_n.24, f32[1024,100]{0,1:T(8,128)S(1)} %fusion.27, pred[2048,1024]{1,0:T(32,128)(4,1)S(1)} %bitcast_compare_fusion.4, bf16[100,2048]{1,0:T(8,128)(2,1)S(1)} %copy-done.3), kind=kOutput, calls=%fused_computation.4.clone.1 | convolution fusion | flops 419635200 | bytes 3768324 | tf_op jit(solution)/shard_map/while/body/eval_jaxpr/dot_general | solution.py:119
  195.2 1.3 bitcast_compare_fusion.4
  197.7 2.9 %fusion.28 = f32[100,8192]{1,0:T(8,128)} fusion(f32[100,8192]{1,0:T(8,128)} %get-tuple-element.304, s32[]{:T(128)S(6)} %select_n.24, f32[1024,100]{0,1:T(8,128)S(1)} %fusion.27, pred[2048,1024]{1,0:T(32,128)(4,1)S(1)} %bitcast_compare_fusion.4, bf16[100,2048]{1,0:T(8,128)(2,1)S(1)} %copy-done.3), kind=kOutput, calls=%fused_computation.4.clone.1 | convolution fusion | flops 419635200 | bytes 3768324 | tf_op jit(solution)/shard_map/while/body/eval_jaxpr/dot_general | solution.py:119
  204.3 2.9 %fusion.28 = f32[100,8192]{1,0:T(8,128)} fusion(f32[100,8192]{1,0:T(8,128)} %get-tuple-element.304, s32[]{:T(128)S(6)} %select_n.24, f32[1024,100]{0,1:T(8,128)S(1)} %fusion.27, pred[2048,1024]{1,0:T(32,128)(4,1)S(1)} %bitcast_compare_fusion.4, bf16[100,2048]{1,0:T(8,128)(2,1)S(1)} %copy-done.3), kind=kOutput, calls=%fused_computation.4.clone.1 | convolution fusion | flops 419635200 | bytes 3768324 | tf_op jit(solution)/shard_map/while/body/eval_jaxpr/dot_general | solution.py:119
  208.3 1.3 bitcast_compare_fusion.4
  210.8 2.9 %fusion.28 = f32[100,8192]{1,0:T(8,128)} fusion(f32[100,8192]{1,0:T(8,128)} %get-tuple-element.304, s32[]{:T(128)S(6)} %select_n.24, f32[1024,100]{0,1:T(8,128)S(1)} %fusion.27, pred[2048,1024]{1,0:T(32,128)(4,1)S(1)} %bitcast_compare_fusion.4, bf16[100,2048]{1,0:T(8,128)(2,1)S(1)} %copy-done.3), kind=kOutput, calls=%fused_computation.4.clone.1 | convolution fusion | flops 419635200 | bytes 3768324 | tf_op jit(solution)/shard_map/while/body/eval_jaxpr/dot_general | solution.py:119
  213.7 4.1 %add.88 = f32[100,8192]{1,0:T(8,128)} add(f32[100,8192]{1,0:T(8,128)S(1)} %copy-done, f32[100,8192]{1,0:T(8,128)} %get-tuple-element.176) | non-fusion elementwise | flops 819200 | bytes 9830400 | tf_op jit(solution)/shard_map/add | solution.py:139
  (135 shorter events, 46.0 us)
Async XLA Ops:
  0.6 3.0 %copy-start = (f32[100,8192]{1,0:T(8,128)S(1)}, f32[100,8192]{1,0:T(8,128)}, u32[]{:S(2)}) copy-start(f32[100,8192]{1,0:T(8,128)} %param.7) | copy-start | bytes 9830404
  3.6 0.8 copy-start.5
  7.9 2.4 %copy-start.1 = (f32[200,2048]{1,0:T(8,128)S(1)}, f32[200,2048]{1,0:T(8,128)}, u32[]{:S(2)}) copy-start(f32[200,2048]{1,0:T(8,128)} %get-tuple-element.279) | copy-start | bytes 4915204 | tf_op jit(solution)/shard_map/while
  13.1 1.2 copy-start.2
  14.3 2.4 %copy-start.1 = (f32[200,2048]{1,0:T(8,128)S(1)}, f32[200,2048]{1,0:T(8,128)}, u32[]{:S(2)}) copy-start(f32[200,2048]{1,0:T(8,128)} %get-tuple-element.279) | copy-start | bytes 4915204 | tf_op jit(solution)/shard_map/while
  19.4 1.2 copy-start.2
  20.7 2.4 %copy-start.1 = (f32[200,2048]{1,0:T(8,128)S(1)}, f32[200,2048]{1,0:T(8,128)}, u32[]{:S(2)}) copy-start(f32[200,2048]{1,0:T(8,128)} %get-tuple-element.279) | copy-start | bytes 4915204 | tf_op jit(solution)/shard_map/while
  25.8 1.2 copy-start.2
  27.1 2.4 %copy-start.1 = (f32[200,2048]{1,0:T(8,128)S(1)}, f32[200,2048]{1,0:T(8,128)}, u32[]{:S(2)}) copy-start(f32[200,2048]{1,0:T(8,128)} %get-tuple-element.279) | copy-start | bytes 4915204 | tf_op jit(solution)/shard_map/while
  32.2 1.2 copy-start.2
  33.5 2.4 %copy-start.1 = (f32[200,2048]{1,0:T(8,128)S(1)}, f32[200,2048]{1,0:T(8,128)}, u32[]{:S(2)}) copy-start(f32[200,2048]{1,0:T(8,128)} %get-tuple-element.279) | copy-start | bytes 4915204 | tf_op jit(solution)/shard_map/while
  38.6 1.2 copy-start.2
  39.9 2.4 %copy-start.1 = (f32[200,2048]{1,0:T(8,128)S(1)}, f32[200,2048]{1,0:T(8,128)}, u32[]{:S(2)}) copy-start(f32[200,2048]{1,0:T(8,128)} %get-tuple-element.279) | copy-start | bytes 4915204 | tf_op jit(solution)/shard_map/while
  45.0 1.2 copy-start.2
  46.3 2.4 %copy-start.1 = (f32[200,2048]{1,0:T(8,128)S(1)}, f32[200,2048]{1,0:T(8,128)}, u32[]{:S(2)}) copy-start(f32[200,2048]{1,0:T(8,128)} %get-tuple-element.279) | copy-start | bytes 4915204 | tf_op jit(solution)/shard_map/while
  51.4 1.2 copy-start.2
  52.7 2.4 %copy-start.1 = (f32[200,2048]{1,0:T(8,128)S(1)}, f32[200,2048]{1,0:T(8,128)}, u32[]{:S(2)}) copy-start(f32[200,2048]{1,0:T(8,128)} %get-tuple-element.279) | copy-start | bytes 4915204 | tf_op jit(solution)/shard_map/while
  57.8 1.2 copy-start.2
  121.9 28.6 %all-to-all-start.3 = ((f32[8,16,3200]{2,1,0:T(8,128)}), f32[8,16,3200]{2,1,0:T(8,128)}, u32[]{:S(2)}, u32[]{:S(2)}) async-start(f32[8,16,3200]{2,1,0:T(8,128)} %broadcast_in_dim.33), calls=%async_computation.3 | async-start | bytes 3276800 | tf_op jit(solution)/shard_map/all_to_all | solution.py:41
  161.5 2.3 %copy-start.4 = (bf16[100,2048]{1,0:T(8,128)(2,1)S(1)}, bf16[100,2048]{1,0:T(8,128)(2,1)}, u32[]{:S(2)}) copy-start(bf16[100,2048]{1,0:T(8,128)(2,1)} %get-tuple-element.315) | copy-start | bytes 1228804 | tf_op jit(solution)/shard_map/while
  163.9 1.2 copy-start.3
  168.1 2.3 %copy-start.4 = (bf16[100,2048]{1,0:T(8,128)(2,1)S(1)}, bf16[100,2048]{1,0:T(8,128)(2,1)}, u32[]{:S(2)}) copy-start(bf16[100,2048]{1,0:T(8,128)(2,1)} %get-tuple-element.315) | copy-start | bytes 1228804 | tf_op jit(solution)/shard_map/while
  170.4 1.2 copy-start.3
  174.6 2.3 %copy-start.4 = (bf16[100,2048]{1,0:T(8,128)(2,1)S(1)}, bf16[100,2048]{1,0:T(8,128)(2,1)}, u32[]{:S(2)}) copy-start(bf16[100,2048]{1,0:T(8,128)(2,1)} %get-tuple-element.315) | copy-start | bytes 1228804 | tf_op jit(solution)/shard_map/while
  176.9 1.2 copy-start.3
  181.1 2.3 %copy-start.4 = (bf16[100,2048]{1,0:T(8,128)(2,1)S(1)}, bf16[100,2048]{1,0:T(8,128)(2,1)}, u32[]{:S(2)}) copy-start(bf16[100,2048]{1,0:T(8,128)(2,1)} %get-tuple-element.315) | copy-start | bytes 1228804 | tf_op jit(solution)/shard_map/while
  183.5 1.2 copy-start.3
  187.7 2.3 %copy-start.4 = (bf16[100,2048]{1,0:T(8,128)(2,1)S(1)}, bf16[100,2048]{1,0:T(8,128)(2,1)}, u32[]{:S(2)}) copy-start(bf16[100,2048]{1,0:T(8,128)(2,1)} %get-tuple-element.315) | copy-start | bytes 1228804 | tf_op jit(solution)/shard_map/while
  190.0 1.2 copy-start.3
  194.2 2.3 %copy-start.4 = (bf16[100,2048]{1,0:T(8,128)(2,1)S(1)}, bf16[100,2048]{1,0:T(8,128)(2,1)}, u32[]{:S(2)}) copy-start(bf16[100,2048]{1,0:T(8,128)(2,1)} %get-tuple-element.315) | copy-start | bytes 1228804 | tf_op jit(solution)/shard_map/while
  196.5 1.2 copy-start.3
  200.7 2.3 %copy-start.4 = (bf16[100,2048]{1,0:T(8,128)(2,1)S(1)}, bf16[100,2048]{1,0:T(8,128)(2,1)}, u32[]{:S(2)}) copy-start(bf16[100,2048]{1,0:T(8,128)(2,1)} %get-tuple-element.315) | copy-start | bytes 1228804 | tf_op jit(solution)/shard_map/while
  203.1 1.2 copy-start.3
  207.3 2.3 %copy-start.4 = (bf16[100,2048]{1,0:T(8,128)(2,1)S(1)}, bf16[100,2048]{1,0:T(8,128)(2,1)}, u32[]{:S(2)}) copy-start(bf16[100,2048]{1,0:T(8,128)(2,1)} %get-tuple-element.315) | copy-start | bytes 1228804 | tf_op jit(solution)/shard_map/while
  209.6 1.2 copy-start.3
where the time goes:
time: 219 us; the launch traced here: 218 us
  matrix products  54.5 us (25%)
  blocking collectives  52.4 us (24%)
  local copies, waits for them, and re-layouts  42 us (19%)
  other arithmetic  39.1 us (18%)
  waiting for transfers between devices  21.4 us (10%)
  starting transfers between devices  7.15 us (3%)
    all_to_all x1, blocking collectives, sent_and_summed(): lax.all_to_all(in_blocks(shard, dim, length), axis, 0, 0, tiled=True)  28.3 us
    dot_general x8, matrix products, apply_advance(): jnp.dot(low_part, one_hot, preferred_element_type=jnp.float32)  23.5 us
    dot_general x8, matrix products, local_advance(): lax.dot_general(partial_value, one_hot, (((1,), (1,)), ((), ())), preferr...  21.7 us
    eq x16, other arithmetic, leaf_table(): matches = id_block[:, None, :] == leaf_slot  21.5 us
    all_to_all x1, waiting for transfers between devices, from_everyone(): lax.all_to_all(jnp.broadcast_to(shard[None], (length, *shard.shape)), axi...  21.4 us
    dynamic_slice x16, local copies, waits for them, and re-layouts, leaf_table(): id_block = lax.dynamic_slice_in_dim(tree_ids, first_row, width, 1)  16 us
    all_to_all x1, blocking collectives, sum_by_axis(): lax.all_to_all(nearer, far, split_axis=0, concat_axis=0, tiled=True)  13.9 us
    all_to_all x1, blocking collectives, from_everyone(): lax.all_to_all(jnp.broadcast_to(shard[None], (length, *shard.shape)), axi...  10.2 us
  transfers between devices with their start and end apart: 1, of which 1 were waited for; matrix products, arithmetic and copies ran while one was open for 0% of the time, Pallas kernels for 0%

commit v1 on v0

v1 whole, which is shorter than its diff:
```python
import functools
import jax, jax.numpy as jnp
from jax import lax
from jax.experimental import pallas as pl
from jax.experimental.pallas import tpu as pltpu
LEAVES=64
STEP=0.5
RIDGE=1.0
F32=jnp.float32; BF=jnp.bfloat16

def turned(b):
    return (b//4%4)*16+(b%4)*4+b//16

def softmax_piece(x, lab):
    m=jnp.max(x,axis=0,keepdims=True)
    e=jnp.exp(x-m)
    s=jnp.sum(e,axis=0,keepdims=True)
    p=e*(1.0/s)
    cls=lax.broadcasted_iota(jnp.int32,x.shape,0)
    g=jnp.where(cls==lab,p-1.0,p)
    h=p*(1.0-p)
    return g.astype(BF),h.astype(BF)

def one_hot(ids, iotas):
    f=ids.astype(F32)
    out=[]
    one=jnp.ones(iotas[0].shape,BF); zero=jnp.zeros(iotas[0].shape,BF)
    for t in range(f.shape[0]):
        r=jnp.broadcast_to(f[t:t+1,:],iotas[0].shape).astype(BF)
        for io in iotas:
            out.append(jnp.where(r==io,one,zero))
    return jnp.concatenate(out,axis=0)

def hist_kernel(UN, pred, lab, ids, out, xbuf, lbuf, ibuf, gh, acc, sems):
    classes,rows=pred.shape
    trees=ids.shape[0]
    NP=8; W=rows//NP
    cps=[pltpu.make_async_copy(pred.at[:,pl.ds(i*W,W)],xbuf.at[:,pl.ds(i*W,W)],sems.at[i]) for i in range(NP)]
    cl=pltpu.make_async_copy(lab,lbuf,sems.at[NP])
    ci=pltpu.make_async_copy(ids,ibuf,sems.at[NP+1])
    cl.start()
    for c in cps: c.start()
    ci.start()
    gh[...]=jnp.zeros_like(gh)
    cl.wait()
    for i in range(NP):
        cps[i].wait()
        @pl.loop(0,W,step=512)
        def _(o):
            sl=pl.ds(pl.multiple_of(i*W+o,512),512)
            g,h=softmax_piece(xbuf[:,sl],lbuf[:,sl])
            gh[0:classes,sl]=g
            gh[128:128+classes,sl]=h
    ci.wait()
    KT=256
    iotas=[(lax.broadcasted_iota(jnp.int32,(16,KT),0)+16*j).astype(F32).astype(BF) for j in range(4)]
    for c in range(trees//8):
        acc[...]=jnp.zeros_like(acc)
        @pl.loop(0,rows,step=KT*UN)
        def _(k):
            tot=None
            for u in range(UN):
                sl=pl.ds(pl.multiple_of(k+u*KT,KT),KT)
                oh=one_hot(ibuf[c*8:c*8+8,sl],iotas)
                d=lax.dot_general(oh,gh[:,sl],(((1,),(1,)),((),())),preferred_element_type=F32)
                tot=d if tot is None else tot+d
            acc[...]+=tot
        out[0,c*512:c*512+512,:]=acc[:,0:128]
        for b in range(64):
            to=c*512+turned(b)*8
            out[1,to:to+8,:]=acc[b*8:b*8+8,128:256]

def hist(pred,lab,ids,UN=8):
    classes,rows=pred.shape; trees=ids.shape[0]
    return pl.pallas_call(
        functools.partial(hist_kernel,UN),
        out_shape=jax.ShapeDtypeStruct((2,trees*LEAVES,128),F32),
        in_specs=[pl.BlockSpec(memory_space=pl.ANY)]*3,
        out_specs=pl.BlockSpec(memory_space=pltpu.VMEM),
        scratch_shapes=[pltpu.VMEM((classes,rows),F32),pltpu.VMEM((1,rows),jnp.int32),pltpu.VMEM((trees,rows),jnp.int32),
            pltpu.VMEM((256,rows),BF),pltpu.VMEM((512,256),F32),pltpu.SemaphoreType.DMA((10,))],
        compiler_params=pltpu.CompilerParams(vmem_limit_bytes=50<<20),
        name='hist',
    )(pred,lab,ids)

def apply_kernel(UN, v, pred, ids, out, own, vt, xbuf, ibuf, obuf, sems, osem):
    classes,rows=pred.shape
    trees=ids.shape[0]
    n=trees*LEAVES
    NP=8; W=rows//NP
    ci=pltpu.make_async_copy(ids,ibuf,sems.at[NP])
    ci.start()
    cps=[pltpu.make_async_copy(pred.at[:,pl.ds(i*W,W)],xbuf.at[:,pl.ds(i*W,W)],sems.at[i]) for i in range(NP)]
    for c in cps: c.start()
    for b in range(n//256):
        vt[:,b*256:b*256+256]=v[b*256:b*256+256,:].T[0:112,:].astype(BF)
    wide=own.shape[1]
    for b in range(wide//128):
        first=pl.multiple_of(lax.axis_index("leaf")*wide+b*128,128)
        own[:,b*128:b*128+128]=v[pl.ds(first,128),:].T[0:classes,:]
    ci.wait()
    KT=256
    iotas=[(lax.broadcasted_iota(jnp.int32,(16,KT),0)+16*j).astype(F32).astype(BF) for j in range(4)]
    outs=[]
    for i in range(NP):
        cps[i].wait()
        @pl.loop(0,W,step=KT)
        def _(o):
            sl=pl.ds(pl.multiple_of(i*W+o,KT),KT)
            tot=None
            for c in range(trees//8):
                oh=one_hot(ibuf[c*8:c*8+8,sl],iotas)
                d=jnp.dot(vt[:,c*512:c*512+512],oh,preferred_element_type=F32)
                tot=d if tot is None else tot+d
            obuf[:,sl]=xbuf[:,sl]+tot[0:classes]
        sl=pl.ds(i*W,W)
        oc=pltpu.make_async_copy(obuf.at[:,sl],out.at[:,sl],osem.at[i])
        oc.start(); outs.append(oc)
    for o in outs: o.wait()

def apply(v,pred,ids,UN=1):
    classes,rows=pred.shape; trees=ids.shape[0]
    return pl.pallas_call(
        functools.partial(apply_kernel,UN),
        out_shape=(jax.ShapeDtypeStruct(pred.shape,F32),jax.ShapeDtypeStruct((classes,trees*LEAVES//lax.axis_size("leaf")),F32)),
        in_specs=[pl.BlockSpec(memory_space=pltpu.VMEM)]+[pl.BlockSpec(memory_space=pl.ANY)]*2,
        out_specs=(pl.BlockSpec(memory_space=pl.ANY),pl.BlockSpec(memory_space=pltpu.VMEM)),
        scratch_shapes=[pltpu.VMEM((112,trees*LEAVES),BF),pltpu.VMEM((classes,rows),F32),pltpu.VMEM((trees,rows),jnp.int32),
            pltpu.VMEM((classes,rows),F32),pltpu.SemaphoreType.DMA((9,)),pltpu.SemaphoreType.DMA((8,))],
        compiler_params=pltpu.CompilerParams(vmem_limit_bytes=50<<20),
        name='apply',
    )(v,pred,ids)

from jax.sharding import Mesh
from jax.sharding import PartitionSpec as P

AXES = ("dp_0", "dp_1", "dp_2", "leaf")
ROWS_OF = (128, 32, 8)


def places():
    y, x, core, z = (lax.axis_index(name) for name in AXES)
    return x, y, z, core


def picks(axis):
    return (1 - axis) * (2 - axis) // 2, axis * (2 - axis), axis * (axis - 1) // 2


def along(axis, step):
    x, y, z, core = places()
    px, py, pz = picks(axis)
    q = px * x + py * y + pz * z
    move = (q + step) % 4 - q
    return (y + py * move, x + px * move, core, z + pz * move)


def spot(axis):
    x, y, z, core = places()
    px, py, pz = picks(axis)
    return px * x + py * y + pz * z


def greet():
    barrier = pltpu.get_barrier_semaphore()
    x, y, z, core = places()
    peers = [along(a, d) for a in range(3) for d in (1, 2, 3)] + [(y, x, 1 - core, z)]
    for peer in peers:
        pl.semaphore_signal(barrier, inc=1, device_id=peer, device_id_type=pl.DeviceIdType.MESH)
    pl.semaphore_wait(barrier, len(peers))


def stages(c, sums, held, bufs, send, recv):
    paired, part_a, got_a, part_b, got_b, part_c, got_c, both = bufs
    x, y, z, core = places()
    axes = [(2 * c + core + p) % 3 for p in range(3)]
    spots = [spot(a) for a in axes]
    base, values = c * 512, held.at[c]
    partner = (y, x, 1 - core, z)

    def copy(i, src, dst, peer):
        return pltpu.make_async_remote_copy(
            src_ref=src, dst_ref=dst, send_sem=send.at[c, i], recv_sem=recv.at[c, i],
            device_id=peer, device_id_type=pl.DeviceIdType.MESH)

    todo = []
    first = copy(0, sums.at[1 - core, pl.ds(base, 512)], paired.at[c], partner)
    todo.append([first])

    def halve(p, part, got):
        rows = ROWS_OF[p]
        out = []
        for d in (1, 2, 3):
            there = (spots[p] + d) % 4
            src = part.at[c, pl.ds(pl.multiple_of(there * rows, rows), rows)]
            out.append(copy(3 * p + d, src, got.at[c, d - 1], along(axes[p], d)))
        return out

    def mine(p, part, got):
        rows = ROWS_OF[p]
        held = part[c, pl.ds(pl.multiple_of(spots[p] * rows, rows), rows)]
        return (held + got[c, 0]) + (got[c, 1] + got[c, 2])

    a, b, e = halve(0, part_a, got_a), halve(1, part_b, got_b), halve(2, part_c, got_c)
    swap = [copy(10, both.at[c, core], both.at[c, core], partner)]
    at = [spots[0] * 128, spots[0] * 128 + spots[1] * 32]
    at.append(at[1] + spots[2] * 8)

    def spread(p):
        rows = ROWS_OF[p]
        where = values.at[pl.ds(pl.multiple_of(at[p], rows), rows)]
        return [copy(10 + 3 * (2 - p) + d, where, where, along(axes[p], d)) for d in (1, 2, 3)]

    def add_pair():
        part_a[c] = sums[core, base:base + 512] + paired[c]

    def add_a():
        part_b[c] = mine(0, part_a, got_a)

    def add_b():
        part_c[c] = mine(1, part_b, got_b)

    def add_c():
        both[c, core] = mine(2, part_c, got_c)

    def solve():
        held[c, pl.ds(pl.multiple_of(at[2], 8), 8)] = -STEP * both[c, 0] / (both[c, 1] + RIDGE)

    steps = [([first], add_pair), (a, add_a), (b, add_b), (e, add_c), (swap, solve),
             (spread(2), None), (spread(1), None), (spread(0), None)]
    return steps


def sum_kernel(sums, values, *scratch):
    held, bufs, send, recv = scratch[0], scratch[1:-2], scratch[-2], scratch[-1]
    greet()
    chunks = [stages(c, sums, held, bufs, send, recv) for c in range(4)]
    for s in range(len(chunks[0])):
        for steps in chunks:
            for copy in steps[s][0]:
                copy.start()
        for steps in chunks:
            for copy in steps[s][0]:
                copy.wait_recv()
            if steps[s][1] is not None:
                steps[s][1]()
    core = lax.axis_index(AXES[2])
    for c in range(4):
        for b in range(64):
            place = pl.multiple_of((b + core * (turned(b) - b)) * 8, 8)
            values[c * 512 + b * 8:c * 512 + b * 8 + 8] = held[c, pl.ds(place, 8)]
    for steps in chunks:
        for copies, _ in steps:
            for copy in copies:
                copy.wait_send()


def total(sums):
    n = sums.shape[1]
    k = n // 512
    return pl.pallas_call(
        sum_kernel,
        out_shape=jax.ShapeDtypeStruct((n, 128), F32),
        in_specs=[pl.BlockSpec(memory_space=pltpu.VMEM)],
        out_specs=pl.BlockSpec(memory_space=pltpu.VMEM),
        scratch_shapes=[
            pltpu.VMEM((k, 512, 128), F32), pltpu.VMEM((k, 512, 128), F32), pltpu.VMEM((k, 512, 128), F32), pltpu.VMEM((k, 3, 128, 128), F32),
            pltpu.VMEM((k, 128, 128), F32), pltpu.VMEM((k, 3, 32, 128), F32),
            pltpu.VMEM((k, 32, 128), F32), pltpu.VMEM((k, 3, 8, 128), F32), pltpu.VMEM((k, 2, 8, 128), F32),
            pltpu.SemaphoreType.DMA((k, 20)), pltpu.SemaphoreType.DMA((k, 20)),
        ],
        compiler_params=pltpu.CompilerParams(collective_id=0, has_side_effects=True, vmem_limit_bytes=24 << 20),
        name='total',
    )(sums)


def shards(predict, labels, leaf_ids):
    sums = hist(predict, labels[None, :], leaf_ids)
    values = total(sums)
    return apply(values, predict, leaf_ids)


def solution(mesh):
    finer = Mesh(mesh.devices.reshape(4, 4, 2, mesh.shape["leaf"]), AXES)
    in_specs = (P(None, AXES), P(AXES), P(None, AXES))
    out_specs = (P(None, AXES), P(None, "leaf"))
    return jax.shard_map(shards, mesh=finer, in_specs=in_specs, out_specs=out_specs, check_vma=False)
```

time: 219 us -> 71.7 us (0.33)
  Pallas kernels: 0 us -> 68.9 us
  matrix products: 54.5 us -> 0 us
  blocking collectives: 52.4 us -> 0 us
  local copies, waits for them, and re-layouts: 42 us -> 1.98 us
  other arithmetic: 39.1 us -> 0 us
  waiting for transfers between devices: 21.4 us -> 0 us
  starting transfers between devices: 7.15 us -> 0 us
    pallas_call x0 -> x3, Pallas kernels: none -> 68.9 us  [the longest x1 40.7 us: total(): pl.pallas_call(sum_kernel, out_shape=jax.ShapeDtypeStruct((n, 128), F32),...]
    dot_general x24 -> x0, matrix products: 54.5 us -> none  [the longest x8 23.5 us: apply_advance(): jnp.dot(low_part, one_hot, preferred_element_type=jnp.float32)]
    all_to_all x3 -> x0, blocking collectives: 52.4 us -> none  [the longest x1 28.3 us: sent_and_summed(): lax.all_to_all(in_blocks(shard, dim, length), axis, 0, 0, tiled=True)]
    eq x16 -> x0, other arithmetic: 21.5 us -> none  [leaf_table(): matches = id_block[:, None, :] == leaf_slot]
    all_to_all x1 -> x0, waiting for transfers between devices: 21.4 us -> none  [from_everyone(): lax.all_to_all(jnp.broadcast_to(shard[None], (length, *shard.shape)), axi...]
    dynamic_slice x17 -> x0, local copies, waits for them, and re-layouts: 17.7 us -> none  [the longest x16 16 us: leaf_table(): id_block = lax.dynamic_slice_in_dim(tree_ids, first_row, width, 1)]
    while x64 -> x0, local copies, waits for them, and re-layouts: 9.53 us -> none
    all_to_all x1 -> x0, starting transfers between devices: 7.15 us -> none  [from_everyone(): lax.all_to_all(jnp.broadcast_to(shard[None], (length, *shard.shape)), axi...]
  transfers between devices with their start and end apart: 1 -> 0, of which waited for: 1 -> 0; matrix products, arithmetic and copies ran while one was open for 0% -> 0% of each run, Pallas kernels for 0% -> 0%
where the time goes in v1:
time: 71.7 us; the launch traced here: 71.5 us
  Pallas kernels  68.9 us (96%)
  local copies, waits for them, and re-layouts  1.98 us (3%)
    pallas_call x1, Pallas kernels, total(): pl.pallas_call(sum_kernel, out_shape=jax.ShapeDtypeStruct((n, 128), F32),...  40.7 us
    pallas_call x1, Pallas kernels, hist(): pl.pallas_call(functools.partial(hist_kernel, UN), out_shape=jax.ShapeDty...  15.2 us
    pallas_call x1, Pallas kernels, apply(): pl.pallas_call(functools.partial(apply_kernel, UN), out_shape=(jax.ShapeD...  13 us
    unnamed x6, local copies, waits for them, and re-layouts  1.98 us

profile of v1, /device:TPU:1, one launch (start us, length us, event | category | flops | bytes accessed | tf_op | source)
XLA Modules:
  0.0 71.5 jit_solution(6633421254113853753)
XLA Ops:
  0.6 0.0 copy-start
  0.6 1.2 %copy-done = s32[32,8192]{1,0:T(8,128)S(1)} copy-done((s32[32,8192]{1,0:T(8,128)S(1)}, s32[32,8192]{1,0:T(8,128)}, u32[]{:S(2)}) %copy-start) | copy-done | bytes 1048600
  1.9 0.0 copy-start.2
  1.9 0.8 %copy-done.2 = s32[8192]{0:T(1024)S(1)} copy-done((s32[8192]{0:T(1024)S(1)}, s32[8192]{0:T(1024)}, u32[]{:S(2)}) %copy-start.2) | copy-done | bytes 32792
  2.6 0.0 copy-start.1
  2.6 15.2 %hist.1.sums = f32[2,2048,128]{2,1,0:T(8,128)S(1)} custom-call(f32[100,8192]{1,0:T(8,128)} %pred_.3, s32[1,8192]{1,0:T(1,128)S(1)} %bitcast.1, s32[32,8192]{1,0:T(8,128)S(1)} %copy-done), custom_call_target="tpu_custom_call" | custom-call | tf_op jit(solution)/shard_map/hist/pallas_call | solution.py:75
  17.8 40.7 %total.1.v = f32[2048,128]{1,0:T(8,128)S(1)} custom-call(f32[2,2048,128]{2,1,0:T(8,128)S(1)} %hist.1.sums), custom_call_target="tpu_custom_call" | custom-call | tf_op jit(solution)/shard_map/total/pallas_call | solution.py:261
  58.5 0.0 copy-done.1
  58.5 13.0 %apply.1 = (f32[100,8192]{1,0:T(8,128)}, f32[100,512]{1,0:T(8,128)}) custom-call(f32[2048,128]{1,0:T(8,128)S(1)} %total.1.v, f32[100,8192]{1,0:T(8,128)} %pred_.3, s32[32,8192]{1,0:T(8,128)S(1)} %copy-done.1), custom_call_target="tpu_custom_call" | custom-call | tf_op jit(solution)/shard_map/apply/pallas_call | solution.py:123
Async XLA Ops:
  0.6 1.2 %copy-start = (s32[32,8192]{1,0:T(8,128)S(1)}, s32[32,8192]{1,0:T(8,128)}, u32[]{:S(2)}) copy-start(s32[32,8192]{1,0:T(8,128)} %ids.3) | copy-start | bytes 3145732
  1.9 0.8 %copy-start.2 = (s32[8192]{0:T(1024)S(1)}, s32[8192]{0:T(1024)}, u32[]{:S(2)}) copy-start(s32[8192]{0:T(1024)} %param.4) | copy-start | bytes 98308
  2.6 55.9 %copy-start.1 = (s32[32,8192]{1,0:T(8,128)S(1)}, s32[32,8192]{1,0:T(8,128)}, u32[]{:S(2)}) copy-start(s32[32,8192]{1,0:T(8,128)} %ids.3) | copy-start | bytes 3145732

commit v2 on v0

v2 whole, which is shorter than its diff:
```python
import jax
import jax.numpy as jnp
from jax import lax
from jax.experimental import pallas as pl
from jax.experimental.pallas import tpu as pltpu
from jax.sharding import Mesh
from jax.sharding import PartitionSpec as P

F32, BF16 = jnp.float32, jnp.bfloat16
LEAVES = 64
AXES = ("dp_0", "dp_1", "dp_2", "leaf")
TREES_AT_ONCE = 8
WIDE = TREES_AT_ONCE * LEAVES
LANES = 128
ROWS_OF = (128, 32, 8)
COPIES = 23
TILE = 256
PIECES = 8

step_size = 0.5
ridge_term = 1.0


def turned(block):
    return (block // 4 % 4) * 16 + (block % 4) * 4 + block // 16


def places():
    y, x, core, z = (lax.axis_index(name) for name in AXES)
    return x, y, z, core


def picks(axis):
    return (1 - axis) * (2 - axis) // 2, axis * (2 - axis), axis * (axis - 1) // 2


def spot(axis):
    x, y, z, _ = places()
    px, py, pz = picks(axis)
    return px * x + py * y + pz * z


def along(axis, step, core):
    x, y, z, _ = places()
    px, py, pz = picks(axis)
    q = spot(axis)
    move = (q + step) % 4 - q
    return (y + py * move, x + px * move, core, z + pz * move)


def partner():
    x, y, z, core = places()
    return (y, x, 1 - core, z)


def greeted():
    core = lax.axis_index(AXES[2])
    return [along(a, d, k) for a in range(3) for d in (1, 2, 3) for k in (core, 1 - core)] + [partner()]


def greet():
    barrier = pltpu.get_barrier_semaphore()
    for peer in greeted():
        pl.semaphore_signal(barrier, inc=1, device_id=peer, device_id_type=pl.DeviceIdType.MESH)


def wait_for_all():
    pl.semaphore_wait(pltpu.get_barrier_semaphore(), len(greeted()))


class Exchange:
    def __init__(self, c, sums, held, bufs, send, recv):
        paired, part_a, got_a, part_b, got_b, part_c, last = bufs
        core = lax.axis_index(AXES[2])
        axes = [(2 * c + core + p) % 3 for p in range(3)]
        spots = [spot(a) for a in axes]
        base, values = c * WIDE, held.at[c]

        def copy(i, src, dst, peer):
            return pltpu.make_async_remote_copy(
                src_ref=src,
                dst_ref=dst,
                send_sem=send.at[c, i],
                recv_sem=recv.at[c, i],
                device_id=peer,
                device_id_type=pl.DeviceIdType.MESH,
            )

        def block(p, step):
            there = (spots[p] + step) % 4
            return pl.ds(pl.multiple_of(there * ROWS_OF[p], ROWS_OF[p]), ROWS_OF[p])

        def halve(p, part, got):
            return [
                copy(3 * p + d, part.at[c, block(p, d)], got.at[c, d - 1], along(axes[p], d, core))
                for d in (1, 2, 3)
            ]

        def mine(p, part, got):
            return (part[c, block(p, 0)] + got[c, 0]) + (got[c, 1] + got[c, 2])

        at = [spots[0] * 128, spots[0] * 128 + spots[1] * 32]
        at.append(at[1] + spots[2] * 8)

        def spread(p):
            where = values.at[pl.ds(pl.multiple_of(at[p], ROWS_OF[p]), ROWS_OF[p])]
            return [copy(14 + 3 * (2 - p) + d - 1, where, where, along(axes[p], d, core)) for d in (1, 2, 3)]

        finals = [copy(7, part_c.at[c, block(2, 0)], last.at[c, core, 0], partner())]
        for d in (1, 2, 3):
            src, dst = part_c.at[c, block(2, d)], last.at[c, core, d]
            finals.append(copy(7 + d, src, dst, along(axes[2], d, core)))
            finals.append(copy(10 + d, src, dst, along(axes[2], d, 1 - core)))

        def add_pair():
            part_a[c] = sums[core, base : base + WIDE] + paired[c]

        def add_a():
            part_b[c] = mine(0, part_a, got_a)

        def add_b():
            part_c[c] = mine(1, part_b, got_b)
            last[c, core, 0] = part_c[c, block(2, 0)]

        def solve():
            grad, hess = (
                (last[c, k, 0] + last[c, k, 1]) + (last[c, k, 2] + last[c, k, 3]) for k in (0, 1)
            )
            held[c, pl.ds(pl.multiple_of(at[2], 8), 8)] = -step_size * grad / (hess + ridge_term)

        first = copy(0, sums.at[1 - core, pl.ds(base, WIDE)], paired.at[c], partner())
        self.steps = [
            ([first], add_pair),
            (halve(0, part_a, got_a), add_a),
            (halve(1, part_b, got_b), add_b),
            (finals, solve),
            (spread(2), None),
            (spread(1), None),
            (spread(0), None),
        ]
        self.now = 0

    @property
    def done(self):
        return self.now == len(self.steps)

    def start(self):
        for copy in self.steps[self.now][0]:
            copy.start()

    def advance(self):
        copies, then = self.steps[self.now]
        for copy in copies:
            copy.wait_recv()
        if then is not None:
            then()
        self.now += 1
        if not self.done:
            self.start()

    def settle(self):
        for copies, _ in self.steps:
            for copy in copies:
                copy.wait_send()


def gradients(predict, labels):
    exponent = jnp.exp(predict - jnp.max(predict, axis=0, keepdims=True))
    probability = exponent * (1.0 / jnp.sum(exponent, axis=0, keepdims=True))
    classes = lax.broadcasted_iota(jnp.int32, predict.shape, 0)
    gradient = jnp.where(classes == labels, probability - 1.0, probability)
    return gradient.astype(BF16), (probability * (1.0 - probability)).astype(BF16)


def leaf_slots(width):
    return [(lax.broadcasted_iota(jnp.int32, (16, width), 0) + 16 * j).astype(F32).astype(BF16) for j in range(4)]


def one_hot(ids, slots):
    shape = slots[0].shape
    one, zero = jnp.ones(shape, BF16), jnp.zeros(shape, BF16)
    ids = ids.astype(F32)
    rows = []
    for t in range(ids.shape[0]):
        held = jnp.broadcast_to(ids[t : t + 1], shape).astype(BF16)
        rows += [jnp.where(held == slot, one, zero) for slot in slots]
    return jnp.concatenate(rows, axis=0)


def chunk_sums(c, ids, stacked, acc, sums, unroll=8):
    rows = ids.shape[1]
    slots = leaf_slots(TILE)
    acc[...] = jnp.zeros_like(acc)

    @pl.loop(0, rows, step=TILE * unroll)
    def _(first):
        total = None
        for u in range(unroll):
            cols = pl.ds(pl.multiple_of(first + u * TILE, TILE), TILE)
            matches = one_hot(ids[c * TREES_AT_ONCE : (c + 1) * TREES_AT_ONCE, cols], slots)
            part = lax.dot_general(
                matches, stacked[:, cols], (((1,), (1,)), ((), ())), preferred_element_type=F32
            )
            total = part if total is None else total + part
        acc[...] += total

    base = c * WIDE
    sums[0, base : base + WIDE] = acc[:, :LANES]
    for b in range(64):
        to = base + turned(b) * 8
        sums[1, to : to + 8] = acc[b * 8 : b * 8 + 8, LANES:]


def in_order(c, held, values):
    core = lax.axis_index(AXES[2])
    for b in range(64):
        place = pl.multiple_of((b + core * (turned(b) - b)) * 8, 8)
        values[c * WIDE + b * 8 : c * WIDE + b * 8 + 8] = held[c, pl.ds(place, 8)]


def class_major(values, first, table):
    for b in range(WIDE // LANES):
        block = values[first + b * LANES : first + (b + 1) * LANES]
        table[:, b * LANES : (b + 1) * LANES] = block.T[: table.shape[0]].astype(BF16)


def grow_kernel(predict, labels, ids, carried, values, *scratch):
    lbuf, ibuf, stacked, acc, table, sums, held = scratch[:7]
    bufs, send, recv, sems = scratch[7:-3], *scratch[-3:]
    classes, rows = predict.shape
    width = rows // PIECES
    greet()
    reads = []
    for i in range(PIECES):
        cols = pl.ds(i * width, width)
        reads.append(pltpu.make_async_copy(predict.at[:, cols], carried.at[:, cols], sems.at[i]))
    labels_read = pltpu.make_async_copy(labels, lbuf, sems.at[PIECES])
    ids_read = pltpu.make_async_copy(ids, ibuf, sems.at[PIECES + 1])
    labels_read.start()
    for read in reads:
        read.start()
    ids_read.start()
    for k in (0, 1):
        stacked[k * LANES + 96 : (k + 1) * LANES] = jnp.zeros((LANES - 96, rows), BF16)
    labels_read.wait()
    for i in range(PIECES):
        reads[i].wait()

        @pl.loop(0, width, step=512)
        def _(first):
            cols = pl.ds(pl.multiple_of(i * width + first, 512), 512)
            gradient, hessian = gradients(carried[:, cols], lbuf[:, cols])
            stacked[:classes, cols] = gradient
            stacked[LANES : LANES + classes, cols] = hessian

    ids_read.wait()
    chunks = [Exchange(c, sums, held, bufs, send, recv) for c in range(ids.shape[0] // TREES_AT_ONCE)]

    def apply(c):
        in_order(c, held, values)
        class_major(values, c * WIDE, table)
        slots = leaf_slots(TILE)

        @pl.loop(0, rows, step=2 * TILE)
        def _(first):
            for u in range(2):
                cols = pl.ds(pl.multiple_of(first + u * TILE, TILE), TILE)
                matches = one_hot(ibuf[c * TREES_AT_ONCE : (c + 1) * TREES_AT_ONCE, cols], slots)
                update = jnp.dot(table[...], matches, preferred_element_type=F32)
                carried[:, cols] += update[:classes]

    newest = len(chunks) - 1
    for c in range(len(chunks)):
        chunk_sums(c, ibuf, stacked, acc, sums)
        if c == 0:
            wait_for_all()
        chunks[c].start()
        for older in reversed(range(c)):
            if c < newest or older == newest - 1:
                chunks[older].advance()
    applied = 0
    while not chunks[newest].done:
        chunks[newest].advance()
        for older in reversed(range(newest)):
            if not chunks[older].done:
                chunks[older].advance()
        if applied < newest and chunks[applied].done:
            apply(applied)
            applied += 1
    while applied < newest:
        apply(applied)
        applied += 1
    in_order(newest, held, values)
    for chunk in chunks:
        chunk.settle()


def grow(predict, labels, ids):
    classes, rows = predict.shape
    leaves = ids.shape[0] * LEAVES
    k = leaves // WIDE
    pinned = [pltpu.with_memory_space_constraint(a, pltpu.HBM) for a in (predict, labels, ids)]
    return pl.pallas_call(
        grow_kernel,
        out_shape=(jax.ShapeDtypeStruct(predict.shape, F32), jax.ShapeDtypeStruct((leaves, LANES), F32)),
        in_specs=[pl.BlockSpec(memory_space=pltpu.HBM)] * 3,
        out_specs=(pl.BlockSpec(memory_space=pltpu.VMEM), pl.BlockSpec(memory_space=pltpu.VMEM)),
        scratch_shapes=[
            pltpu.VMEM((1, rows), jnp.int32),
            pltpu.VMEM(ids.shape, jnp.int32),
            pltpu.VMEM((2 * LANES, rows), BF16),
            pltpu.VMEM((WIDE, 2 * LANES), F32),
            pltpu.VMEM((112, WIDE), BF16),
            pltpu.VMEM((2, leaves, LANES), F32),
            pltpu.VMEM((k, WIDE, LANES), F32),
            pltpu.VMEM((k, WIDE, LANES), F32),
            pltpu.VMEM((k, WIDE, LANES), F32),
            pltpu.VMEM((k, 3, 128, LANES), F32),
            pltpu.VMEM((k, 128, LANES), F32),
            pltpu.VMEM((k, 3, 32, LANES), F32),
            pltpu.VMEM((k, 32, LANES), F32),
            pltpu.VMEM((k, 2, 4, 8, LANES), F32),
            pltpu.SemaphoreType.DMA((k, COPIES)),
            pltpu.SemaphoreType.DMA((k, COPIES)),
            pltpu.SemaphoreType.DMA((PIECES + 2,)),
        ],
        compiler_params=pltpu.CompilerParams(
            collective_id=0, has_side_effects=True, vmem_limit_bytes=40 << 20
        ),
        name="grow",
    )(*pinned)


def finish_kernel(values, carried, ids, out, own, table, ibuf, obuf, sems, ids_sem):
    classes, rows = carried.shape
    width = rows // PIECES
    first_id = ids.shape[0] - TREES_AT_ONCE
    ids_read = pltpu.make_async_copy(ids.at[pl.ds(first_id, TREES_AT_ONCE)], ibuf, ids_sem)
    ids_read.start()
    class_major(values, values.shape[0] - WIDE, table)
    ids_read.wait()
    slots = leaf_slots(TILE)
    writes = []
    for i in range(PIECES):

        @pl.loop(0, width, step=2 * TILE)
        def _(first):
            for u in range(2):
                cols = pl.ds(pl.multiple_of(i * width + first + u * TILE, TILE), TILE)
                matches = one_hot(ibuf[:, cols], slots)
                update = jnp.dot(table[...], matches, preferred_element_type=F32)
                obuf[:, cols] = carried[:, cols] + update[:classes]

        cols = pl.ds(i * width, width)
        writes.append(pltpu.make_async_copy(obuf.at[:, cols], out.at[:, cols], sems.at[i]))
        writes[-1].start()
    own_width = own.shape[1]
    for b in range(own_width // LANES):
        first = pl.multiple_of(lax.axis_index("leaf") * own_width + b * LANES, LANES)
        own[:, b * LANES : (b + 1) * LANES] = values[pl.ds(first, LANES)].T[:classes]
    for write in writes:
        write.wait()


def finish(values, carried, ids):
    classes, rows = carried.shape
    own_width = values.shape[0] // lax.axis_size("leaf")
    return pl.pallas_call(
        finish_kernel,
        out_shape=(
            jax.ShapeDtypeStruct(carried.shape, F32),
            jax.ShapeDtypeStruct((classes, own_width), F32),
        ),
        in_specs=[
            pl.BlockSpec(memory_space=pltpu.VMEM),
            pl.BlockSpec(memory_space=pltpu.VMEM),
            pl.BlockSpec(memory_space=pl.ANY),
        ],
        out_specs=(pl.BlockSpec(memory_space=pl.ANY), pl.BlockSpec(memory_space=pltpu.VMEM)),
        scratch_shapes=[
            pltpu.VMEM((112, WIDE), BF16),
            pltpu.VMEM((TREES_AT_ONCE, rows), jnp.int32),
            pltpu.VMEM((classes, rows), F32),
            pltpu.SemaphoreType.DMA((PIECES,)),
            pltpu.SemaphoreType.DMA,
        ],
        compiler_params=pltpu.CompilerParams(vmem_limit_bytes=24 << 20),
        name="finish",
    )(values, carried, ids)


def shards(predict, labels, leaf_ids):
    carried, values = grow(predict, labels[None, :], leaf_ids)
    return finish(values, carried, leaf_ids)


def solution(mesh):
    finer = Mesh(mesh.devices.reshape(4, 4, 2, mesh.shape["leaf"]), AXES)
    in_specs = (P(None, AXES), P(AXES), P(None, AXES))
    out_specs = (P(None, AXES), P(None, "leaf"))
    return jax.shard_map(shards, mesh=finer, in_specs=in_specs, out_specs=out_specs, check_vma=False)
```

time: 219 us -> 65.7 us (0.30)
  the two profiles are of different devices: /device:TPU:1 before, /device:TPU:0 now
where the time goes in v2:
time: 65.7 us; the launch traced here: 65.6 us
  Pallas kernels  64.9 us (99%)
    pallas_call x1, Pallas kernels, grow(): pl.pallas_call(grow_kernel, out_shape=(jax.ShapeDtypeStruct(predict.shape...  59.4 us
    pallas_call x1, Pallas kernels, finish(): pl.pallas_call(finish_kernel, out_shape=(jax.ShapeDtypeStruct(carried.sha...  5.56 us

profile of v2, /device:TPU:0, one launch (start us, length us, event | category | flops | bytes accessed | tf_op | source)
XLA Modules:
  0.0 65.6 jit_solution(10051528804585542731)
XLA Ops:
  0.6 0.0 copy-start
  0.6 59.4 %grow.1 = (f32[100,8192]{1,0:T(8,128)S(1)}, f32[2048,128]{1,0:T(8,128)S(1)}) custom-call(f32[100,8192]{1,0:T(8,128)} %predict.1, s32[1,8192]{1,0:T(1,128)} %bitcast.1, s32[32,8192]{1,0:T(8,128)} %ids.3), custom_call_target="tpu_custom_call" | custom-call | tf_op jit(solution)/shard_map/grow/pallas_call | solution.py:303
  60.0 0.0 copy-done
  60.0 5.6 %finish.1 = (f32[100,8192]{1,0:T(8,128)}, f32[100,512]{1,0:T(8,128)}) custom-call(f32[2048,128]{1,0:T(8,128)S(1)} %get-tuple-element.4.values, f32[100,8192]{1,0:T(8,128)S(1)} %get-tuple-element.5.carried, s32[32,8192]{1,0:T(8,128)S(1)} %copy-done), custom_call_target="tpu_custom_call" | custom-call | tf_op jit(solution)/shard_map/finish/pallas_call | solution.py:368
Async XLA Ops:
  0.6 59.4 %copy-start = (s32[32,8192]{1,0:T(8,128)S(1)}, s32[32,8192]{1,0:T(8,128)}, u32[]{:S(2)}) copy-start(s32[32,8192]{1,0:T(8,128)} %ids.3) | copy-start | bytes 3145732

commit v3 on v2

--- a/solution.py
+++ b/solution.py
@@ -16,6 +16,8 @@
 COPIES = 23
 TILE = 256
 PIECES = 8
+APPLY = 16
+WRITES = 4
 
 step_size = 0.5
 ridge_term = 1.0
@@ -187,12 +189,13 @@
     return jnp.concatenate(rows, axis=0)
 
 
-def chunk_sums(c, ids, stacked, acc, sums, unroll=8):
-    rows = ids.shape[1]
+def chunk_sums(c, half, ids, stacked, acc, sums, unroll=8):
+    rows = ids.shape[1] // 2
     slots = leaf_slots(TILE)
-    acc[...] = jnp.zeros_like(acc)
-
-    @pl.loop(0, rows, step=TILE * unroll)
+    if half == 0:
+        acc[...] = jnp.zeros_like(acc)
+
+    @pl.loop(half * rows, (half + 1) * rows, step=TILE * unroll)
     def _(first):
         total = None
         for u in range(unroll):
@@ -204,11 +207,12 @@
             total = part if total is None else total + part
         acc[...] += total
 
-    base = c * WIDE
-    sums[0, base : base + WIDE] = acc[:, :LANES]
-    for b in range(64):
-        to = base + turned(b) * 8
-        sums[1, to : to + 8] = acc[b * 8 : b * 8 + 8, LANES:]
+    if half == 1:
+        base = c * WIDE
+        sums[0, base : base + WIDE] = acc[:, :LANES]
+        for b in range(64):
+            to = base + turned(b) * 8
+            sums[1, to : to + 8] = acc[b * 8 : b * 8 + 8, LANES:]
 
 
 def in_order(c, held, values):
@@ -261,35 +265,31 @@
         class_major(values, c * WIDE, table)
         slots = leaf_slots(TILE)
 
-        @pl.loop(0, rows, step=2 * TILE)
+        @pl.loop(0, rows, step=APPLY * TILE)
         def _(first):
-            for u in range(2):
+            for u in range(APPLY):
                 cols = pl.ds(pl.multiple_of(first + u * TILE, TILE), TILE)
                 matches = one_hot(ibuf[c * TREES_AT_ONCE : (c + 1) * TREES_AT_ONCE, cols], slots)
                 update = jnp.dot(table[...], matches, preferred_element_type=F32)
                 carried[:, cols] += update[:classes]
 
     newest = len(chunks) - 1
-    for c in range(len(chunks)):
-        chunk_sums(c, ibuf, stacked, acc, sums)
+    for c in range(newest + 1):
+        chunk_sums(c, 0, ibuf, stacked, acc, sums)
+        if c >= 1:
+            chunks[c - 1].advance()
+        chunk_sums(c, 1, ibuf, stacked, acc, sums)
         if c == 0:
             wait_for_all()
+        if c >= 2:
+            chunks[c - 2].advance()
         chunks[c].start()
-        for older in reversed(range(c)):
-            if c < newest or older == newest - 1:
-                chunks[older].advance()
-    applied = 0
     while not chunks[newest].done:
-        chunks[newest].advance()
-        for older in reversed(range(newest)):
-            if not chunks[older].done:
-                chunks[older].advance()
-        if applied < newest and chunks[applied].done:
-            apply(applied)
-            applied += 1
-    while applied < newest:
-        apply(applied)
-        applied += 1
+        for c in (newest, 0, *range(newest - 1, 0, -1)):
+            if not chunks[c].done:
+                chunks[c].advance()
+                if chunks[c].done and c < newest:
+                    apply(c)
     in_order(newest, held, values)
     for chunk in chunks:
         chunk.settle()
@@ -333,7 +333,7 @@
 
 def finish_kernel(values, carried, ids, out, own, table, ibuf, obuf, sems, ids_sem):
     classes, rows = carried.shape
-    width = rows // PIECES
+    width = rows // WRITES
     first_id = ids.shape[0] - TREES_AT_ONCE
     ids_read = pltpu.make_async_copy(ids.at[pl.ds(first_id, TREES_AT_ONCE)], ibuf, ids_sem)
     ids_read.start()
@@ -341,16 +341,11 @@
     ids_read.wait()
     slots = leaf_slots(TILE)
     writes = []
-    for i in range(PIECES):
-
-        @pl.loop(0, width, step=2 * TILE)
-        def _(first):
-            for u in range(2):
-                cols = pl.ds(pl.multiple_of(i * width + first + u * TILE, TILE), TILE)
-                matches = one_hot(ibuf[:, cols], slots)
-                update = jnp.dot(table[...], matches, preferred_element_type=F32)
-                obuf[:, cols] = carried[:, cols] + update[:classes]
-
+    for i in range(WRITES):
+        for u in range(width // TILE):
+            cols = pl.ds(i * width + u * TILE, TILE)
+            update = jnp.dot(table[...], one_hot(ibuf[:, cols], slots), preferred_element_type=F32)
+            obuf[:, cols] = carried[:, cols] + update[:classes]
         cols = pl.ds(i * width, width)
         writes.append(pltpu.make_async_copy(obuf.at[:, cols], out.at[:, cols], sems.at[i]))
         writes[-1].start()
@@ -381,7 +376,7 @@
             pltpu.VMEM((112, WIDE), BF16),
             pltpu.VMEM((TREES_AT_ONCE, rows), jnp.int32),
             pltpu.VMEM((classes, rows), F32),
-            pltpu.SemaphoreType.DMA((PIECES,)),
+            pltpu.SemaphoreType.DMA((WRITES,)),
             pltpu.SemaphoreType.DMA,
         ],
         compiler_params=pltpu.CompilerParams(vmem_limit_bytes=24 << 20),

time: 65.7 us -> 54.5 us (0.83)
  the two profiles are of different devices: /device:TPU:0 before, /device:TPU:1 now
where the time goes in v3:
time: 54.5 us; the launch traced here: 53.7 us
  Pallas kernels  53 us (97%)
  between operations  0.65 us (1%)
    pallas_call x1, Pallas kernels, grow(): pl.pallas_call(grow_kernel, out_shape=(jax.ShapeDtypeStruct(predict.shape...  49.9 us
    pallas_call x1, Pallas kernels, finish(): pl.pallas_call(finish_kernel, out_shape=(jax.ShapeDtypeStruct(carried.sha...  3.07 us

profile of v3, /device:TPU:1, one launch (start us, length us, event | category | flops | bytes accessed | tf_op | source)
XLA Modules:
  0.0 53.7 jit_solution(17448744301434923167)
XLA Ops:
  0.6 0.0 copy-start
  0.6 49.9 %grow.1 = (f32[100,8192]{1,0:T(8,128)S(1)}, f32[2048,128]{1,0:T(8,128)S(1)}) custom-call(f32[100,8192]{1,0:T(8,128)} %predict.1, s32[1,8192]{1,0:T(1,128)} %bitcast.1, s32[32,8192]{1,0:T(8,128)} %ids.3), custom_call_target="tpu_custom_call" | custom-call | tf_op jit(solution)/shard_map/grow/pallas_call | solution.py:303
  50.6 0.0 copy-done
  50.6 3.1 %finish.1 = (f32[100,8192]{1,0:T(8,128)}, f32[100,512]{1,0:T(8,128)}) custom-call(f32[2048,128]{1,0:T(8,128)S(1)} %get-tuple-element.4.values, f32[100,8192]{1,0:T(8,128)S(1)} %get-tuple-element.5.carried, s32[32,8192]{1,0:T(8,128)S(1)} %copy-done), custom_call_target="tpu_custom_call" | custom-call | tf_op jit(solution)/shard_map/finish/pallas_call | solution.py:363
Async XLA Ops:
  0.6 50.0 %copy-start = (s32[32,8192]{1,0:T(8,128)S(1)}, s32[32,8192]{1,0:T(8,128)}, u32[]{:S(2)}) copy-start(s32[32,8192]{1,0:T(8,128)} %ids.3) | copy-start | bytes 3145732

commit v4 on v3

v4 whole, which is shorter than its diff:
```python
import jax
import jax.numpy as jnp
from jax import lax
from jax.experimental import pallas as pl
from jax.experimental.pallas import tpu as pltpu
from jax.sharding import Mesh
from jax.sharding import PartitionSpec as P

F32, BF16 = jnp.float32, jnp.bfloat16
LEAVES = 64
AXES = ("dp_0", "dp_1", "dp_2", "leaf")
TREES_AT_ONCE = 8
WIDE = TREES_AT_ONCE * LEAVES
LANES = 128
CHUNKS = (8, 8, 8, 8)
COPIES = 24
TILE = 256
PIECES = 8
APPLY = 16
WRITES = 4
UNROLL = 16
HALF_US, APPLY_US, EARLY_US = 1.15, 1.9, 0.3

step_size = 0.5
ridge_term = 1.0


def turned(block):
    return (block // 4 % 4) * 16 + (block % 4) * 4 + block // 16


def places():
    y, x, core, z = (lax.axis_index(name) for name in AXES)
    return x, y, z, core


def picks(axis):
    return (1 - axis) * (2 - axis) // 2, axis * (2 - axis), axis * (axis - 1) // 2


def spot(axis):
    x, y, z, _ = places()
    px, py, pz = picks(axis)
    return px * x + py * y + pz * z


def along(axis, step, core):
    x, y, z, _ = places()
    px, py, pz = picks(axis)
    q = spot(axis)
    move = (q + step) % 4 - q
    return (y + py * move, x + px * move, core, z + pz * move)


def partner():
    x, y, z, core = places()
    return (y, x, 1 - core, z)


def greeted():
    core = lax.axis_index(AXES[2])
    return [along(a, d, k) for a in range(3) for d in (1, 2, 3) for k in (core, 1 - core)] + [partner()]


def greet():
    barrier = pltpu.get_barrier_semaphore()
    for peer in greeted():
        pl.semaphore_signal(barrier, inc=1, device_id=peer, device_id_type=pl.DeviceIdType.MESH)


def wait_for_all():
    pl.semaphore_wait(pltpu.get_barrier_semaphore(), len(greeted()))


class Exchange:
    def __init__(self, c, trees, base, sums, held, bufs, send, recv):
        paired, part_a, got_a, part_b, got_b, part_c, last = bufs
        core = lax.axis_index(AXES[2])
        axes = [(c + core + p) % 3 for p in range(3)]
        spots = [spot(a) for a in axes]
        size = trees * LEAVES
        rows_of = [size // 4, size // 16, size // 64]
        whole = pl.ds(base, size)
        starts = [base, base // 4, base // 16, base // 64]

        def copy(i, src, dst, peer, lands=None):
            return pltpu.make_async_remote_copy(
                src_ref=src,
                dst_ref=dst,
                send_sem=send.at[c, i],
                recv_sem=recv.at[c, i if lands is None else lands],
                device_id=peer,
                device_id_type=pl.DeviceIdType.MESH,
            )

        def block(p, step):
            there = (spots[p] + step) % 4
            return pl.ds(pl.multiple_of(starts[p] + there * rows_of[p], 8), rows_of[p])

        def landing(p):
            return pl.ds(starts[p + 1], rows_of[p])

        def halve(p, part, got):
            return [
                copy(3 * p + d, part.at[block(p, d)], got.at[d - 1, landing(p)], along(axes[p], d, core))
                for d in (1, 2, 3)
            ]

        def mine(p, part, got):
            return (part[block(p, 0)] + got[0, landing(p)]) + (got[1, landing(p)] + got[2, landing(p)])

        at = [base + spots[0] * rows_of[0]]
        for p in (1, 2):
            at.append(at[-1] + spots[p] * rows_of[p])

        def spread(p):
            where = held.at[pl.ds(pl.multiple_of(at[p], 8), rows_of[p])]
            return [copy(14 + 3 * (2 - p) + d - 1, where, where, along(axes[p], d, core)) for d in (1, 2, 3)]

        beside = copy(7, part_c.at[block(2, 0)], last.at[core, 0, landing(2)], partner())
        finals, arrivals = [], []
        for d in (1, 2, 3):
            src, dst = part_c.at[block(2, d)], last.at[core, d, landing(2)]
            peer = along(axes[2], d, 1)
            finals.append(copy(7 + d, src, dst, peer, 10 + d - 3 * core))
            arrivals += [copy(7 + d, src, dst, peer, lands) for lands in (7 + d, 10 + d)]
        forward = copy(23, held.at[whole], held.at[whole], partner())

        def add_pair():
            part_a[whole] = sums[core, whole] + paired[whole]

        def add_a():
            part_b[landing(0)] = mine(0, part_a, got_a)

        def add_b():
            part_c[landing(1)] = mine(1, part_b, got_b)
            last[core, 0, landing(2)] = part_c[block(2, 0)]

        def solve():
            @pl.when(core == 1)
            def _():
                grad, hess = (
                    (last[k, 0, landing(2)] + last[k, 1, landing(2)])
                    + (last[k, 2, landing(2)] + last[k, 3, landing(2)])
                    for k in (0, 1)
                )
                where = pl.ds(pl.multiple_of(at[2], 8), rows_of[2])
                held[where] = -step_size * grad / (hess + ridge_term)

        first = copy(0, sums.at[1 - core, whole], paired.at[whole], partner())
        every = None
        a, b = halve(0, part_a, got_a), halve(1, part_b, got_b)
        self.steps = [
            ([([first], every, [first], every)], add_pair),
            ([(a, every, a, every)], add_a),
            ([(b, every, b, every)], add_b),
            ([(finals, every, arrivals, 1), ([beside], 0, [beside], 1)], solve),
            *(([(out, 1, out, 1)], None) for out in (spread(2), spread(1), spread(0))),
            ([([forward], 1, [forward], 0)], None),
        ]
        self.now = 0

    def start(self):
        for copies, sender, _, _ in self.steps[self.now][0]:
            on(sender, [copy.start for copy in copies])

    def advance(self):
        groups, then = self.steps[self.now]
        for _, _, copies, receiver in groups:
            on(receiver, [copy.wait_recv for copy in copies])
        if then is not None:
            then()
        self.now += 1
        if self.now < len(self.steps):
            self.start()

    def settle(self):
        for groups, _ in self.steps:
            for copies, sender, _, _ in groups:
                on(sender, [copy.wait_send for copy in copies])


def on(core, calls):
    def go():
        for call in calls:
            call()

    if core is None:
        go()
    else:
        pl.when(lax.axis_index(AXES[2]) == core)(go)


def gradients(predict, labels):
    exponent = jnp.exp(predict - jnp.max(predict, axis=0, keepdims=True))
    probability = exponent * (1.0 / jnp.sum(exponent, axis=0, keepdims=True))
    classes = lax.broadcasted_iota(jnp.int32, predict.shape, 0)
    gradient = jnp.where(classes == labels, probability - 1.0, probability)
    return gradient.astype(BF16), (probability * (1.0 - probability)).astype(BF16)


def leaf_slots(width):
    return [(lax.broadcasted_iota(jnp.int32, (16, width), 0) + 16 * j).astype(F32).astype(BF16) for j in range(4)]


def one_hot(ids, slots):
    shape = slots[0].shape
    one, zero = jnp.ones(shape, BF16), jnp.zeros(shape, BF16)
    ids = ids.astype(F32)
    rows = []
    for t in range(ids.shape[0]):
        held = jnp.broadcast_to(ids[t : t + 1], shape).astype(BF16)
        rows += [jnp.where(held == slot, one, zero) for slot in slots]
    return jnp.concatenate(rows, axis=0)


def half_sums(slot, ids, stacked, acc):
    rows = ids.shape[1] // 2
    slots = leaf_slots(TILE)
    trees = pl.ds(pl.multiple_of(slot // 2 * TREES_AT_ONCE, TREES_AT_ONCE), TREES_AT_ONCE)

    @pl.when(slot % 2 == 0)
    def _():
        acc[...] = jnp.zeros_like(acc)

    @pl.loop(0, rows, step=TILE * UNROLL)
    def _(first):
        total = None
        for u in range(UNROLL):
            cols = pl.ds(pl.multiple_of(slot % 2 * rows + first + u * TILE, TILE), TILE)
            matches = one_hot(ids[trees, cols], slots)
            part = lax.dot_general(
                matches, stacked[:, cols], (((1,), (1,)), ((), ())), preferred_element_type=F32
            )
            total = part if total is None else total + part
        acc[...] += total


def keep_sums(c, acc, sums):
    base = pl.multiple_of(c * WIDE, WIDE)
    sums[0, pl.ds(base, WIDE)] = acc[:, :LANES]
    for b in range(64):
        sums[1, pl.ds(base + turned(b) * 8, 8)] = acc[b * 8 : b * 8 + 8, LANES:]


def in_order(c, held, values):
    base = pl.multiple_of(c * WIDE, WIDE)
    for b in range(64):
        values[pl.ds(base + b * 8, 8)] = held[pl.ds(base + turned(b) * 8, 8)]


def class_major(values, first, table):
    for b in range(table.shape[1] // LANES):
        block = values[pl.ds(first + b * LANES, LANES)]
        table[:, b * LANES : (b + 1) * LANES] = block.T[: table.shape[0]].astype(BF16)


def plan():
    steps = lambda m: (1.5 + 0.4 * m, 3.5 + m, 3.5 + 0.3 * m, 3.5, 3.0, 3.0 + 0.3 * m, 3.0 + m, 1.5)
    ends = [sum(CHUNKS[: c + 1]) // TREES_AT_ONCE for c in range(len(CHUNKS))]
    newest = len(CHUNKS) - 1
    order, clock, due, now = [], 0.0, {}, {}
    waiting = []

    def advance(c):
        nonlocal clock
        clock = max(clock, due[c]) + 0.15
        now[c] += 1
        order.append(("advance", c))
        lengths = steps(CHUNKS[c] // TREES_AT_ONCE)
        if now[c] < len(lengths):
            due[c] = clock + lengths[now[c]]
        else:
            del due[c]
            waiting.append(c)

    for group in range(ends[-1]):
        for half in (0, 1):
            order.append(("sums", group, half))
            clock += HALF_US
            if half and group + 1 in ends:
                c = ends.index(group + 1)
                order.append(("start", c))
                now[c], due[c] = 0, clock + steps(CHUNKS[c] // TREES_AT_ONCE)[0]
            for c in sorted(due, key=due.get):
                if due[c] <= clock + EARLY_US:
                    advance(c)
    while newest in due:
        c = min(due, key=lambda c: due[c] - (0.3 if c == newest else 0.0))
        if waiting and due[c] - clock > APPLY_US * CHUNKS[waiting[0]] / 8 * 0.6:
            order.append(("apply", waiting.pop(0)))
            clock += APPLY_US * CHUNKS[order[-1][1]] / 8
        else:
            advance(c)
    order += [("advance", c) for c in due for _ in range(now[c], 8)]
    waiting += list(due)
    return order + [("apply", c) for c in waiting if c != newest]


def grow_kernel(predict, labels, ids, carried, values, *scratch):
    lbuf, ibuf, stacked, acc, table, sums, held = scratch[:7]
    bufs, send, recv, sems = scratch[7:-3], *scratch[-3:]
    classes, rows = predict.shape
    width = rows // PIECES
    greet()

    def read(i):
        cols = pl.ds(pl.multiple_of(i * width, width), width)
        return pltpu.make_async_copy(predict.at[:, cols], carried.at[:, cols], sems.at[i])

    labels_read = pltpu.make_async_copy(labels, lbuf, sems.at[PIECES])
    ids_read = pltpu.make_async_copy(ids, ibuf, sems.at[PIECES + 1])
    labels_read.start()
    for i in range(PIECES):
        read(i).start()
    ids_read.start()
    for k in (0, 1):
        stacked[k * LANES + 96 : (k + 1) * LANES] = jnp.zeros((LANES - 96, rows), BF16)
    labels_read.wait()

    @pl.loop(0, PIECES)
    def _(i):
        read(i).wait()

        @pl.loop(0, width, step=512)
        def _(first):
            cols = pl.ds(pl.multiple_of(i * width + first, 512), 512)
            gradient, hessian = gradients(carried[:, cols], lbuf[:, cols])
            stacked[:classes, cols] = gradient
            stacked[LANES : LANES + classes, cols] = hessian

    ids_read.wait()
    bases = [sum(CHUNKS[:c]) * LEAVES for c in range(len(CHUNKS))]
    chunks = [Exchange(c, CHUNKS[c], bases[c], sums, held, bufs, send, recv) for c in range(len(CHUNKS))]

    def apply(c):
        in_order(c, held, values)
        class_major(values, pl.multiple_of(c * WIDE, WIDE), table)
        slots = leaf_slots(TILE)
        trees = pl.ds(pl.multiple_of(c * TREES_AT_ONCE, TREES_AT_ONCE), TREES_AT_ONCE)

        @pl.loop(0, rows, step=APPLY * TILE)
        def _(first):
            for u in range(APPLY):
                cols = pl.ds(pl.multiple_of(first + u * TILE, TILE), TILE)
                update = jnp.dot(table[...], one_hot(ibuf[trees, cols], slots), preferred_element_type=F32)
                carried[:, cols] += update[:classes]

    def exchange(actions):
        for what, c in actions:
            getattr(chunks[c], what)()

    parts = [[]]
    for action in plan():
        if action[0] in ("sums", "apply"):
            parts.append([])
        else:
            parts[-1].append(action)
    halves = 2 * len(chunks)

    @pl.loop(0, halves)
    def _(slot):
        half_sums(slot, ibuf, stacked, acc)

        @pl.when(slot % 2 == 1)
        def _():
            keep_sums(slot // 2, acc, sums)

        for k in range(halves - 1):
            if parts[k + 1]:

                @pl.when(slot == k)
                def _():
                    if k == 1:
                        wait_for_all()
                    exchange(parts[k + 1])

    exchange(parts[halves])

    @pl.loop(0, len(chunks) - 1)
    def _(c):
        apply(c)
        for k in range(len(chunks) - 1):
            if parts[halves + 1 + k]:

                @pl.when(c == k)
                def _():
                    exchange(parts[halves + 1 + k])

    in_order(len(chunks) - 1, held, values)
    for chunk in chunks:
        chunk.settle()


def grow(predict, labels, ids):
    classes, rows = predict.shape
    leaves = ids.shape[0] * LEAVES
    k = len(CHUNKS)
    pinned = [pltpu.with_memory_space_constraint(a, pltpu.HBM) for a in (predict, labels, ids)]
    return pl.pallas_call(
        grow_kernel,
        out_shape=(jax.ShapeDtypeStruct(predict.shape, F32), jax.ShapeDtypeStruct((leaves, LANES), F32)),
        in_specs=[pl.BlockSpec(memory_space=pltpu.HBM)] * 3,
        out_specs=(pl.BlockSpec(memory_space=pltpu.VMEM), pl.BlockSpec(memory_space=pltpu.VMEM)),
        scratch_shapes=[
            pltpu.VMEM((1, rows), jnp.int32),
            pltpu.VMEM(ids.shape, jnp.int32),
            pltpu.VMEM((2 * LANES, rows), BF16),
            pltpu.VMEM((WIDE, 2 * LANES), F32),
            pltpu.VMEM((112, WIDE), BF16),
            pltpu.VMEM((2, leaves, LANES), F32),
            pltpu.VMEM((leaves, LANES), F32),
            pltpu.VMEM((leaves, LANES), F32),
            pltpu.VMEM((leaves, LANES), F32),
            pltpu.VMEM((3, leaves // 4, LANES), F32),
            pltpu.VMEM((leaves // 4, LANES), F32),
            pltpu.VMEM((3, leaves // 16, LANES), F32),
            pltpu.VMEM((leaves // 16, LANES), F32),
            pltpu.VMEM((2, 4, leaves // 64, LANES), F32),
            pltpu.SemaphoreType.DMA((k, COPIES)),
            pltpu.SemaphoreType.DMA((k, COPIES)),
            pltpu.SemaphoreType.DMA((PIECES + 2,)),
        ],
        compiler_params=pltpu.CompilerParams(
            collective_id=0, has_side_effects=True, vmem_limit_bytes=40 << 20
        ),
        name="grow",
    )(*pinned)


def finish_kernel(values, carried, ids, out, own, table, ibuf, obuf, sems, ids_sem):
    classes, rows = carried.shape
    width = rows // WRITES
    first_id = ids.shape[0] - CHUNKS[-1]
    ids_read = pltpu.make_async_copy(ids.at[pl.ds(first_id, CHUNKS[-1])], ibuf, ids_sem)
    ids_read.start()
    class_major(values, first_id * LEAVES, table)
    ids_read.wait()
    slots = leaf_slots(TILE)
    writes = []
    for i in range(WRITES):
        for u in range(width // TILE):
            cols = pl.ds(i * width + u * TILE, TILE)
            update = jnp.dot(table[...], one_hot(ibuf[:, cols], slots), preferred_element_type=F32)
            obuf[:, cols] = carried[:, cols] + update[:classes]
        cols = pl.ds(i * width, width)
        writes.append(pltpu.make_async_copy(obuf.at[:, cols], out.at[:, cols], sems.at[i]))
        writes[-1].start()
    own_width = own.shape[1]
    for b in range(own_width // LANES):
        first = pl.multiple_of(lax.axis_index("leaf") * own_width + b * LANES, LANES)
        own[:, b * LANES : (b + 1) * LANES] = values[pl.ds(first, LANES)].T[:classes]
    for write in writes:
        write.wait()


def finish(values, carried, ids):
    classes, rows = carried.shape
    own_width = values.shape[0] // lax.axis_size("leaf")
    return pl.pallas_call(
        finish_kernel,
        out_shape=(
            jax.ShapeDtypeStruct(carried.shape, F32),
            jax.ShapeDtypeStruct((classes, own_width), F32),
        ),
        in_specs=[
            pl.BlockSpec(memory_space=pltpu.VMEM),
            pl.BlockSpec(memory_space=pltpu.VMEM),
            pl.BlockSpec(memory_space=pl.ANY),
        ],
        out_specs=(pl.BlockSpec(memory_space=pl.ANY), pl.BlockSpec(memory_space=pltpu.VMEM)),
        scratch_shapes=[
            pltpu.VMEM((112, CHUNKS[-1] * LEAVES), BF16),
            pltpu.VMEM((CHUNKS[-1], rows), jnp.int32),
            pltpu.VMEM((classes, rows), F32),
            pltpu.SemaphoreType.DMA((WRITES,)),
            pltpu.SemaphoreType.DMA,
        ],
        compiler_params=pltpu.CompilerParams(vmem_limit_bytes=24 << 20),
        name="finish",
    )(values, carried, ids)


def shards(predict, labels, leaf_ids):
    carried, values = grow(predict, labels[None, :], leaf_ids)
    return finish(values, carried, leaf_ids)


def solution(mesh):
    finer = Mesh(mesh.devices.reshape(4, 4, 2, mesh.shape["leaf"]), AXES)
    in_specs = (P(None, AXES), P(AXES), P(None, AXES))
    out_specs = (P(None, AXES), P(None, "leaf"))
    return jax.shard_map(shards, mesh=finer, in_specs=in_specs, out_specs=out_specs, check_vma=False)
```

time: 54.5 us -> 49.4 us (0.906); the launches traced: 53.7 us -> 49.3 us
  Pallas kernels: 53 us -> 48.7 us
    pallas_call x1, Pallas kernels: 49.9 us -> 45.6 us  [grow(): pl.pallas_call(grow_kernel, out_shape=(jax.ShapeDtypeStruct(predict.shape...]
where the time goes in v4:
time: 49.4 us; the launch traced here: 49.3 us
  Pallas kernels  48.7 us (99%)
  between operations  0.65 us (1%)
    pallas_call x1, Pallas kernels, grow(): pl.pallas_call(grow_kernel, out_shape=(jax.ShapeDtypeStruct(predict.shape...  45.6 us
    pallas_call x1, Pallas kernels, finish(): pl.pallas_call(finish_kernel, out_shape=(jax.ShapeDtypeStruct(carried.sha...  3.07 us

profile of v4, /device:TPU:1, one launch (start us, length us, event | category | flops | bytes accessed | tf_op | source)
XLA Modules:
  0.0 49.3 jit_solution(10636397010692683776)
XLA Ops:
  0.6 0.0 copy-start
  0.6 45.6 %grow.1 = (f32[100,8192]{1,0:T(8,128)S(1)}, f32[2048,128]{1,0:T(8,128)S(1)}) custom-call(f32[100,8192]{1,0:T(8,128)} %predict.1, s32[1,8192]{1,0:T(1,128)} %bitcast.1, s32[32,8192]{1,0:T(8,128)} %ids.3), custom_call_target="tpu_custom_call" | custom-call | tf_op jit(solution)/shard_map/grow/pallas_call | solution.py:400
  46.3 0.0 copy-done
  46.3 3.1 %finish.1 = (f32[100,8192]{1,0:T(8,128)}, f32[100,512]{1,0:T(8,128)}) custom-call(f32[2048,128]{1,0:T(8,128)S(1)} %get-tuple-element.4.values, f32[100,8192]{1,0:T(8,128)S(1)} %get-tuple-element.5.carried, s32[32,8192]{1,0:T(8,128)S(1)} %copy-done), custom_call_target="tpu_custom_call" | custom-call | tf_op jit(solution)/shard_map/finish/pallas_call | solution.py:460
Async XLA Ops:
  0.6 45.6 %copy-start = (s32[32,8192]{1,0:T(8,128)S(1)}, s32[32,8192]{1,0:T(8,128)}, u32[]{:S(2)}) copy-start(s32[32,8192]{1,0:T(8,128)} %ids.3) | copy-start | bytes 3145732

commit v5 on v4

--- a/solution.py
+++ b/solution.py
@@ -13,7 +13,7 @@
 WIDE = TREES_AT_ONCE * LEAVES
 LANES = 128
 CHUNKS = (8, 8, 8, 8)
-COPIES = 24
+COPIES = 16
 TILE = 256
 PIECES = 8
 APPLY = 16
@@ -57,9 +57,16 @@
     return (y, x, 1 - core, z)
 
 
+def everywhere(core):
+    x, y, z, _ = places()
+    moves = [(a, b, c) for a in range(4) for b in range(4) for c in range(4)][1:]
+    moves.sort(key=lambda move: -sum(min(m, 4 - m) for m in move))
+    return [((y + b) % 4, (x + a) % 4, core, (z + c) % 4) for a, b, c in moves]
+
+
 def greeted():
     core = lax.axis_index(AXES[2])
-    return [along(a, d, k) for a in range(3) for d in (1, 2, 3) for k in (core, 1 - core)] + [partner()]
+    return everywhere(core) + [along(a, d, 1 - core) for a in range(3) for d in (1, 2, 3)] + [partner()]
 
 
 def greet():
@@ -109,13 +116,8 @@
         def mine(p, part, got):
             return (part[block(p, 0)] + got[0, landing(p)]) + (got[1, landing(p)] + got[2, landing(p)])
 
-        at = [base + spots[0] * rows_of[0]]
-        for p in (1, 2):
-            at.append(at[-1] + spots[p] * rows_of[p])
-
-        def spread(p):
-            where = held.at[pl.ds(pl.multiple_of(at[p], 8), rows_of[p])]
-            return [copy(14 + 3 * (2 - p) + d - 1, where, where, along(axes[p], d, core)) for d in (1, 2, 3)]
+        first_row = base + sum(spots[p] * rows_of[p] for p in range(3))
+        where = pl.ds(pl.multiple_of(first_row, 8), rows_of[2])
 
         beside = copy(7, part_c.at[block(2, 0)], last.at[core, 0, landing(2)], partner())
         finals, arrivals = [], []
@@ -124,7 +126,10 @@
             peer = along(axes[2], d, 1)
             finals.append(copy(7 + d, src, dst, peer, 10 + d - 3 * core))
             arrivals += [copy(7 + d, src, dst, peer, lands) for lands in (7 + d, 10 + d)]
-        forward = copy(23, held.at[whole], held.at[whole], partner())
+        rounds = [copy(14, held.at[where], held.at[where], peer) for peer in everywhere(1)]
+        others = pl.ds(base, size - rows_of[2])
+        round_all = [copy(14, held.at[others], held.at[others], partner())]
+        forward = copy(15, held.at[whole], held.at[whole], partner())
 
         def add_pair():
             part_a[whole] = sums[core, whole] + paired[whole]
@@ -144,7 +149,6 @@
                     + (last[k, 2, landing(2)] + last[k, 3, landing(2)])
                     for k in (0, 1)
                 )
-                where = pl.ds(pl.multiple_of(at[2], 8), rows_of[2])
                 held[where] = -step_size * grad / (hess + ridge_term)
 
         first = copy(0, sums.at[1 - core, whole], paired.at[whole], partner())
@@ -155,7 +159,7 @@
             ([(a, every, a, every)], add_a),
             ([(b, every, b, every)], add_b),
             ([(finals, every, arrivals, 1), ([beside], 0, [beside], 1)], solve),
-            *(([(out, 1, out, 1)], None) for out in (spread(2), spread(1), spread(0))),
+            ([(rounds, 1, round_all, 1)], None),
             ([([forward], 1, [forward], 0)], None),
         ]
         self.now = 0
@@ -176,8 +180,9 @@
 
     def settle(self):
         for groups, _ in self.steps:
-            for copies, sender, _, _ in groups:
-                on(sender, [copy.wait_send for copy in copies])
+            for copies, sender, arrivals, _ in groups:
+                out = arrivals if len(arrivals) == 1 else copies
+                on(sender, [copy.wait_send for copy in out])
 
 
 def on(core, calls):
@@ -256,7 +261,7 @@
 
 
 def plan():
-    steps = lambda m: (1.5 + 0.4 * m, 3.5 + m, 3.5 + 0.3 * m, 3.5, 3.0, 3.0 + 0.3 * m, 3.0 + m, 1.5)
+    steps = lambda m: (1.5 + 0.4 * m, 3.5 + m, 3.5 + 0.3 * m, 3.5, 8.0 + 0.5 * m, 1.5)
     ends = [sum(CHUNKS[: c + 1]) // TREES_AT_ONCE for c in range(len(CHUNKS))]
     newest = len(CHUNKS) - 1
     order, clock, due, now = [], 0.0, {}, {}
@@ -292,7 +297,7 @@
             clock += APPLY_US * CHUNKS[order[-1][1]] / 8
         else:
             advance(c)
-    order += [("advance", c) for c in due for _ in range(now[c], 8)]
+    order += [("advance", c) for c in due for _ in range(now[c], 6)]
     waiting += list(due)
     return order + [("apply", c) for c in waiting if c != newest]
 

time: 49.4 us -> 45.4 us (0.919)
  Pallas kernels: 48.7 us -> 44.6 us
    pallas_call x1, Pallas kernels: 45.6 us -> 41.5 us  [grow(): pl.pallas_call(grow_kernel, out_shape=(jax.ShapeDtypeStruct(predict.shape...]
where the time goes in v5:
time: 45.4 us; the launch traced here: 45.2 us
  Pallas kernels  44.6 us (98%)
  between operations  0.65 us (1%)
    pallas_call x1, Pallas kernels, grow(): pl.pallas_call(grow_kernel, out_shape=(jax.ShapeDtypeStruct(predict.shape...  41.5 us
    pallas_call x1, Pallas kernels, finish(): pl.pallas_call(finish_kernel, out_shape=(jax.ShapeDtypeStruct(carried.sha...  3.04 us

profile of v5, /device:TPU:1, one launch (start us, length us, event | category | flops | bytes accessed | tf_op | source)
XLA Modules:
  0.0 45.2 jit_solution(2603744163479678768)
XLA Ops:
  0.6 0.0 copy-start
  0.6 41.5 %grow.1 = (f32[100,8192]{1,0:T(8,128)S(1)}, f32[2048,128]{1,0:T(8,128)S(1)}) custom-call(f32[100,8192]{1,0:T(8,128)} %predict.1, s32[1,8192]{1,0:T(1,128)} %bitcast.1, s32[32,8192]{1,0:T(8,128)} %ids.3), custom_call_target="tpu_custom_call" | custom-call | tf_op jit(solution)/shard_map/grow/pallas_call | solution.py:405
  42.2 0.0 copy-done
  42.2 3.0 %finish.1 = (f32[100,8192]{1,0:T(8,128)}, f32[100,512]{1,0:T(8,128)}) custom-call(f32[2048,128]{1,0:T(8,128)S(1)} %get-tuple-element.4.values, f32[100,8192]{1,0:T(8,128)S(1)} %get-tuple-element.5.carried, s32[32,8192]{1,0:T(8,128)S(1)} %copy-done), custom_call_target="tpu_custom_call" | custom-call | tf_op jit(solution)/shard_map/finish/pallas_call | solution.py:465
Async XLA Ops:
  0.6 41.5 %copy-start = (s32[32,8192]{1,0:T(8,128)S(1)}, s32[32,8192]{1,0:T(8,128)}, u32[]{:S(2)}) copy-start(s32[32,8192]{1,0:T(8,128)} %ids.3) | copy-start | bytes 3145732

commit v6 on v4

--- a/solution.py
+++ b/solution.py
@@ -13,7 +13,7 @@
 WIDE = TREES_AT_ONCE * LEAVES
 LANES = 128
 CHUNKS = (8, 8, 8, 8)
-COPIES = 24
+COPIES = 6
 TILE = 256
 PIECES = 8
 APPLY = 16
@@ -25,63 +25,53 @@
 ridge_term = 1.0
 
 
-def turned(block):
-    return (block // 4 % 4) * 16 + (block % 4) * 4 + block // 16
-
-
 def places():
     y, x, core, z = (lax.axis_index(name) for name in AXES)
     return x, y, z, core
 
 
-def picks(axis):
-    return (1 - axis) * (2 - axis) // 2, axis * (2 - axis), axis * (axis - 1) // 2
-
-
-def spot(axis):
-    x, y, z, _ = places()
-    px, py, pz = picks(axis)
-    return px * x + py * y + pz * z
-
-
-def along(axis, step, core):
-    x, y, z, _ = places()
-    px, py, pz = picks(axis)
-    q = spot(axis)
-    move = (q + step) % 4 - q
-    return (y + py * move, x + px * move, core, z + pz * move)
-
-
 def partner():
     x, y, z, core = places()
     return (y, x, 1 - core, z)
 
 
-def greeted():
-    core = lax.axis_index(AXES[2])
-    return [along(a, d, k) for a in range(3) for d in (1, 2, 3) for k in (core, 1 - core)] + [partner()]
+def moves():
+    found = [(a, b, c) for a in range(4) for b in range(4) for c in range(4)][1:]
+    return sorted(found, key=lambda move: -sum(min(m, 4 - m) for m in move))
+
+
+def chip_at(move, core):
+    x, y, z, _ = places()
+    a, b, c = ((at + m) % 4 for at, m in zip((x, y, z), move))
+    return (b, a, core, c), a * 16 + b * 4 + c
 
 
 def greet():
     barrier = pltpu.get_barrier_semaphore()
-    for peer in greeted():
-        pl.semaphore_signal(barrier, inc=1, device_id=peer, device_id_type=pl.DeviceIdType.MESH)
+
+    def call(core):
+        peers = [partner()] if core == 1 else []
+        for peer in peers + [chip_at(move, core)[0] for move in moves()]:
+            pl.semaphore_signal(barrier, inc=1, device_id=peer, device_id_type=pl.DeviceIdType.MESH)
+
+    call(1)
+
+    @pl.when(lax.axis_index(AXES[2]) == 1)
+    def _():
+        call(0)
 
 
 def wait_for_all():
-    pl.semaphore_wait(pltpu.get_barrier_semaphore(), len(greeted()))
+    pl.semaphore_wait(pltpu.get_barrier_semaphore(), 64 + 63 * lax.axis_index(AXES[2]))
 
 
 class Exchange:
     def __init__(self, c, trees, base, sums, held, bufs, send, recv):
-        paired, part_a, got_a, part_b, got_b, part_c, last = bufs
-        core = lax.axis_index(AXES[2])
-        axes = [(c + core + p) % 3 for p in range(3)]
-        spots = [spot(a) for a in axes]
+        paired, summed, last = bufs
+        x, y, z, core = places()
         size = trees * LEAVES
-        rows_of = [size // 4, size // 16, size // 64]
+        rows = size // 64
         whole = pl.ds(base, size)
-        starts = [base, base // 4, base // 16, base // 64]
 
         def copy(i, src, dst, peer, lands=None):
             return pltpu.make_async_remote_copy(
@@ -93,69 +83,36 @@
                 device_id_type=pl.DeviceIdType.MESH,
             )
 
-        def block(p, step):
-            there = (spots[p] + step) % 4
-            return pl.ds(pl.multiple_of(starts[p] + there * rows_of[p], 8), rows_of[p])
-
-        def landing(p):
-            return pl.ds(starts[p + 1], rows_of[p])
-
-        def halve(p, part, got):
-            return [
-                copy(3 * p + d, part.at[block(p, d)], got.at[d - 1, landing(p)], along(axes[p], d, core))
-                for d in (1, 2, 3)
-            ]
-
-        def mine(p, part, got):
-            return (part[block(p, 0)] + got[0, landing(p)]) + (got[1, landing(p)] + got[2, landing(p)])
-
-        at = [base + spots[0] * rows_of[0]]
-        for p in (1, 2):
-            at.append(at[-1] + spots[p] * rows_of[p])
-
-        def spread(p):
-            where = held.at[pl.ds(pl.multiple_of(at[p], 8), rows_of[p])]
-            return [copy(14 + 3 * (2 - p) + d - 1, where, where, along(axes[p], d, core)) for d in (1, 2, 3)]
-
-        beside = copy(7, part_c.at[block(2, 0)], last.at[core, 0, landing(2)], partner())
-        finals, arrivals = [], []
-        for d in (1, 2, 3):
-            src, dst = part_c.at[block(2, d)], last.at[core, d, landing(2)]
-            peer = along(axes[2], d, 1)
-            finals.append(copy(7 + d, src, dst, peer, 10 + d - 3 * core))
-            arrivals += [copy(7 + d, src, dst, peer, lands) for lands in (7 + d, 10 + d)]
-        forward = copy(23, held.at[whole], held.at[whole], partner())
+        def block(chip):
+            return pl.ds(pl.multiple_of(base + chip * rows, 8), rows)
+
+        own = block(x * 16 + y * 4 + z)
+        pieces, rounds = [], []
+        for n, move in enumerate(moves()):
+            peer, chip = chip_at(move, 1)
+            pieces.append(copy(1, summed.at[block(chip)], last.at[c, core, n], peer, 2 - core))
+            rounds.append(copy(4, held.at[own], held.at[own], peer))
+        others = pl.ds(0, 63)
+        arrived = [copy(1, last.at[c, k, others], last.at[c, k, others], partner(), 2 - k) for k in (0, 1)]
+        beside = copy(3, summed.at[own], last.at[c, 0, 63], partner())
+        rest = held.at[pl.ds(base, size - rows)]
+        first = copy(0, sums.at[1 - core, whole], paired.at[whole], partner())
+        forward = copy(5, held.at[whole], held.at[whole], partner())
 
         def add_pair():
-            part_a[whole] = sums[core, whole] + paired[whole]
-
-        def add_a():
-            part_b[landing(0)] = mine(0, part_a, got_a)
-
-        def add_b():
-            part_c[landing(1)] = mine(1, part_b, got_b)
-            last[core, 0, landing(2)] = part_c[block(2, 0)]
+            summed[whole] = sums[core, whole] + paired[whole]
 
         def solve():
             @pl.when(core == 1)
             def _():
-                grad, hess = (
-                    (last[k, 0, landing(2)] + last[k, 1, landing(2)])
-                    + (last[k, 2, landing(2)] + last[k, 3, landing(2)])
-                    for k in (0, 1)
-                )
-                where = pl.ds(pl.multiple_of(at[2], 8), rows_of[2])
-                held[where] = -step_size * grad / (hess + ridge_term)
-
-        first = copy(0, sums.at[1 - core, whole], paired.at[whole], partner())
-        every = None
-        a, b = halve(0, part_a, got_a), halve(1, part_b, got_b)
+                last[c, 1, 63] = summed[own]
+                grad, hess = (jnp.sum(last[c, k], axis=0) for k in (0, 1))
+                held[own] = -step_size * grad / (hess + ridge_term)
+
         self.steps = [
-            ([([first], every, [first], every)], add_pair),
-            ([(a, every, a, every)], add_a),
-            ([(b, every, b, every)], add_b),
-            ([(finals, every, arrivals, 1), ([beside], 0, [beside], 1)], solve),
-            *(([(out, 1, out, 1)], None) for out in (spread(2), spread(1), spread(0))),
+            ([([first], None, [first], None)], add_pair),
+            ([(pieces, None, arrived, 1), ([beside], 0, [beside], 1)], solve),
+            ([(rounds, 1, [copy(4, rest, rest, partner())], 1)], None),
             ([([forward], 1, [forward], 0)], None),
         ]
         self.now = 0
@@ -176,8 +133,8 @@
 
     def settle(self):
         for groups, _ in self.steps:
-            for copies, sender, _, _ in groups:
-                on(sender, [copy.wait_send for copy in copies])
+            for copies, sender, arrivals, _ in groups:
+                on(sender, [arrivals[0].wait_send])
 
 
 def on(core, calls):
@@ -239,14 +196,7 @@
 def keep_sums(c, acc, sums):
     base = pl.multiple_of(c * WIDE, WIDE)
     sums[0, pl.ds(base, WIDE)] = acc[:, :LANES]
-    for b in range(64):
-        sums[1, pl.ds(base + turned(b) * 8, 8)] = acc[b * 8 : b * 8 + 8, LANES:]
-
-
-def in_order(c, held, values):
-    base = pl.multiple_of(c * WIDE, WIDE)
-    for b in range(64):
-        values[pl.ds(base + b * 8, 8)] = held[pl.ds(base + turned(b) * 8, 8)]
+    sums[1, pl.ds(base, WIDE)] = acc[:, LANES:]
 
 
 def class_major(values, first, table):
@@ -256,7 +206,7 @@
 
 
 def plan():
-    steps = lambda m: (1.5 + 0.4 * m, 3.5 + m, 3.5 + 0.3 * m, 3.5, 3.0, 3.0 + 0.3 * m, 3.0 + m, 1.5)
+    steps = lambda m: (1.5 + 0.4 * m, 8.0 + m, 8.0 + 0.5 * m, 1.5)
     ends = [sum(CHUNKS[: c + 1]) // TREES_AT_ONCE for c in range(len(CHUNKS))]
     newest = len(CHUNKS) - 1
     order, clock, due, now = [], 0.0, {}, {}
@@ -292,7 +242,7 @@
             clock += APPLY_US * CHUNKS[order[-1][1]] / 8
         else:
             advance(c)
-    order += [("advance", c) for c in due for _ in range(now[c], 8)]
+    order += [("advance", c) for c in due for _ in range(now[c], 4)]
     waiting += list(due)
     return order + [("apply", c) for c in waiting if c != newest]
 
@@ -334,8 +284,7 @@
     chunks = [Exchange(c, CHUNKS[c], bases[c], sums, held, bufs, send, recv) for c in range(len(CHUNKS))]
 
     def apply(c):
-        in_order(c, held, values)
-        class_major(values, pl.multiple_of(c * WIDE, WIDE), table)
+        class_major(held, pl.multiple_of(c * WIDE, WIDE), table)
         slots = leaf_slots(TILE)
         trees = pl.ds(pl.multiple_of(c * TREES_AT_ONCE, TREES_AT_ONCE), TREES_AT_ONCE)
 
@@ -387,7 +336,7 @@
                 def _():
                     exchange(parts[halves + 1 + k])
 
-    in_order(len(chunks) - 1, held, values)
+    values[...] = held[...]
     for chunk in chunks:
         chunk.settle()
 
@@ -412,11 +361,7 @@
             pltpu.VMEM((leaves, LANES), F32),
             pltpu.VMEM((leaves, LANES), F32),
             pltpu.VMEM((leaves, LANES), F32),
-            pltpu.VMEM((3, leaves // 4, LANES), F32),
-            pltpu.VMEM((leaves // 4, LANES), F32),
-            pltpu.VMEM((3, leaves // 16, LANES), F32),
-            pltpu.VMEM((leaves // 16, LANES), F32),
-            pltpu.VMEM((2, 4, leaves // 64, LANES), F32),
+            pltpu.VMEM((k, 2, 64, leaves // k // 64, LANES), F32),
             pltpu.SemaphoreType.DMA((k, COPIES)),
             pltpu.SemaphoreType.DMA((k, COPIES)),
             pltpu.SemaphoreType.DMA((PIECES + 2,)),

time: 49.4 us -> 43 us (0.87)
  Pallas kernels: 48.7 us -> 42.3 us
    pallas_call x1, Pallas kernels: 45.6 us -> 39.2 us  [grow(): pl.pallas_call(grow_kernel, out_shape=(jax.ShapeDtypeStruct(predict.shape...]
where the time goes in v6:
time: 43 us; the launch traced here: 42.9 us
  Pallas kernels  42.3 us (98%)
  between operations  0.65 us (2%)
    pallas_call x1, Pallas kernels, grow(): pl.pallas_call(grow_kernel, out_shape=(jax.ShapeDtypeStruct(predict.shape...  39.2 us
    pallas_call x1, Pallas kernels, finish(): pl.pallas_call(finish_kernel, out_shape=(jax.ShapeDtypeStruct(carried.sha...  3.06 us

profile of v6, /device:TPU:1, one launch (start us, length us, event | category | flops | bytes accessed | tf_op | source)
XLA Modules:
  0.0 42.9 jit_solution(16139024941361383341)
XLA Ops:
  0.6 0.0 copy-start
  0.6 39.2 %grow.1 = (f32[100,8192]{1,0:T(8,128)S(1)}, f32[2048,128]{1,0:T(8,128)S(1)}) custom-call(f32[100,8192]{1,0:T(8,128)} %predict.1, s32[1,8192]{1,0:T(1,128)} %bitcast.1, s32[32,8192]{1,0:T(8,128)} %ids.3), custom_call_target="tpu_custom_call" | custom-call | tf_op jit(solution)/shard_map/grow/pallas_call | solution.py:349
  39.9 0.0 copy-done
  39.9 3.1 %finish.1 = (f32[100,8192]{1,0:T(8,128)}, f32[100,512]{1,0:T(8,128)}) custom-call(f32[2048,128]{1,0:T(8,128)S(1)} %get-tuple-element.4.values, f32[100,8192]{1,0:T(8,128)S(1)} %get-tuple-element.5.carried, s32[32,8192]{1,0:T(8,128)S(1)} %copy-done), custom_call_target="tpu_custom_call" | custom-call | tf_op jit(solution)/shard_map/finish/pallas_call | solution.py:405
Async XLA Ops:
  0.6 39.2 %copy-start = (s32[32,8192]{1,0:T(8,128)S(1)}, s32[32,8192]{1,0:T(8,128)}, u32[]{:S(2)}) copy-start(s32[32,8192]{1,0:T(8,128)} %ids.3) | copy-start | bytes 3145732

commit v7 on v6

--- a/solution.py
+++ b/solution.py
@@ -19,7 +19,8 @@
 APPLY = 16
 WRITES = 4
 UNROLL = 16
-HALF_US, APPLY_US, EARLY_US = 1.15, 1.9, 0.3
+SOFTMAX = 1024
+HALF_US, APPLY_US, EARLY_US = 1.15, 1.9, 1.2
 
 step_size = 0.5
 ridge_term = 1.0
@@ -206,7 +207,7 @@
 
 
 def plan():
-    steps = lambda m: (1.5 + 0.4 * m, 8.0 + m, 8.0 + 0.5 * m, 1.5)
+    steps = lambda m: (1.5 + 0.4 * m, 9.0 + m, 8.5 + 0.5 * m, 1.5)
     ends = [sum(CHUNKS[: c + 1]) // TREES_AT_ONCE for c in range(len(CHUNKS))]
     newest = len(CHUNKS) - 1
     order, clock, due, now = [], 0.0, {}, {}
@@ -252,7 +253,6 @@
     bufs, send, recv, sems = scratch[7:-3], *scratch[-3:]
     classes, rows = predict.shape
     width = rows // PIECES
-    greet()
 
     def read(i):
         cols = pl.ds(pl.multiple_of(i * width, width), width)
@@ -264,6 +264,7 @@
     for i in range(PIECES):
         read(i).start()
     ids_read.start()
+    greet()
     for k in (0, 1):
         stacked[k * LANES + 96 : (k + 1) * LANES] = jnp.zeros((LANES - 96, rows), BF16)
     labels_read.wait()
@@ -272,9 +273,9 @@
     def _(i):
         read(i).wait()
 
-        @pl.loop(0, width, step=512)
+        @pl.loop(0, width, step=SOFTMAX)
         def _(first):
-            cols = pl.ds(pl.multiple_of(i * width + first, 512), 512)
+            cols = pl.ds(pl.multiple_of(i * width + first, SOFTMAX), SOFTMAX)
             gradient, hessian = gradients(carried[:, cols], lbuf[:, cols])
             stacked[:classes, cols] = gradient
             stacked[LANES : LANES + classes, cols] = hessian
@@ -284,6 +285,8 @@
     chunks = [Exchange(c, CHUNKS[c], bases[c], sums, held, bufs, send, recv) for c in range(len(CHUNKS))]
 
     def apply(c):
+        chunk = pl.ds(pl.multiple_of(c * WIDE, WIDE), WIDE)
+        values[chunk] = held[chunk]
         class_major(held, pl.multiple_of(c * WIDE, WIDE), table)
         slots = leaf_slots(TILE)
         trees = pl.ds(pl.multiple_of(c * TREES_AT_ONCE, TREES_AT_ONCE), TREES_AT_ONCE)
@@ -336,7 +339,7 @@
                 def _():
                     exchange(parts[halves + 1 + k])
 
-    values[...] = held[...]
+    values[-WIDE:] = held[-WIDE:]
     for chunk in chunks:
         chunk.settle()
 

time: 43 us -> 41.2 us (0.958)
  Pallas kernels: 42.3 us -> 40.4 us
    pallas_call x1, Pallas kernels: 39.2 us -> 37.4 us  [grow(): pl.pallas_call(grow_kernel, out_shape=(jax.ShapeDtypeStruct(predict.shape...]
where the time goes in v7:
time: 41.2 us; the launch traced here: 41.1 us
  Pallas kernels  40.4 us (98%)
  between operations  0.65 us (2%)
    pallas_call x1, Pallas kernels, grow(): pl.pallas_call(grow_kernel, out_shape=(jax.ShapeDtypeStruct(predict.shape...  37.4 us
    pallas_call x1, Pallas kernels, finish(): pl.pallas_call(finish_kernel, out_shape=(jax.ShapeDtypeStruct(carried.sha...  3.04 us

profile of v7, /device:TPU:1, one launch (start us, length us, event | category | flops | bytes accessed | tf_op | source)
XLA Modules:
  0.0 41.1 jit_solution(7403901188793097800)
XLA Ops:
  0.6 0.0 copy-start
  0.6 37.4 %grow.1 = (f32[100,8192]{1,0:T(8,128)S(1)}, f32[2048,128]{1,0:T(8,128)S(1)}) custom-call(f32[100,8192]{1,0:T(8,128)} %predict.1, s32[1,8192]{1,0:T(1,128)} %bitcast.1, s32[32,8192]{1,0:T(8,128)} %ids.3), custom_call_target="tpu_custom_call" | custom-call | tf_op jit(solution)/shard_map/grow/pallas_call | solution.py:352
  38.0 0.0 copy-done
  38.0 3.0 %finish.1 = (f32[100,8192]{1,0:T(8,128)}, f32[100,512]{1,0:T(8,128)}) custom-call(f32[2048,128]{1,0:T(8,128)S(1)} %get-tuple-element.4.values, f32[100,8192]{1,0:T(8,128)S(1)} %get-tuple-element.5.carried, s32[32,8192]{1,0:T(8,128)S(1)} %copy-done), custom_call_target="tpu_custom_call" | custom-call | tf_op jit(solution)/shard_map/finish/pallas_call | solution.py:408
Async XLA Ops:
  0.6 37.4 %copy-start = (s32[32,8192]{1,0:T(8,128)S(1)}, s32[32,8192]{1,0:T(8,128)}, u32[]{:S(2)}) copy-start(s32[32,8192]{1,0:T(8,128)} %ids.3) | copy-start | bytes 3145732

commit v8 on v7

--- a/solution.py
+++ b/solution.py
@@ -16,11 +16,11 @@
 COPIES = 6
 TILE = 256
 PIECES = 8
-APPLY = 16
+APPLY = 32
 WRITES = 4
 UNROLL = 16
 SOFTMAX = 1024
-HALF_US, APPLY_US, EARLY_US = 1.15, 1.9, 1.2
+HALF_US, APPLY_US, EARLY_US = 1.15, 1.9, 0.8
 
 step_size = 0.5
 ridge_term = 1.0

time: 41.2 us -> 41 us (level)
  no operation moved by 1% of the time
where the time goes in v8:
time: 41 us; the launch traced here: 40.9 us
  Pallas kernels  40.3 us (98%)
  between operations  0.65 us (2%)
    pallas_call x1, Pallas kernels, grow(): pl.pallas_call(grow_kernel, out_shape=(jax.ShapeDtypeStruct(predict.shape...  37.2 us
    pallas_call x1, Pallas kernels, finish(): pl.pallas_call(finish_kernel, out_shape=(jax.ShapeDtypeStruct(carried.sha...  3.04 us

profile of v8, /device:TPU:1, one launch (start us, length us, event | category | flops | bytes accessed | tf_op | source)
XLA Modules:
  0.0 40.9 jit_solution(17827452512944504846)
XLA Ops:
  0.6 0.0 copy-start
  0.6 37.2 %grow.1 = (f32[100,8192]{1,0:T(8,128)S(1)}, f32[2048,128]{1,0:T(8,128)S(1)}) custom-call(f32[100,8192]{1,0:T(8,128)} %predict.1, s32[1,8192]{1,0:T(1,128)} %bitcast.1, s32[32,8192]{1,0:T(8,128)} %ids.3), custom_call_target="tpu_custom_call" | custom-call | tf_op jit(solution)/shard_map/grow/pallas_call | solution.py:352
  37.9 0.0 copy-done
  37.9 3.0 %finish.1 = (f32[100,8192]{1,0:T(8,128)}, f32[100,512]{1,0:T(8,128)}) custom-call(f32[2048,128]{1,0:T(8,128)S(1)} %get-tuple-element.4.values, f32[100,8192]{1,0:T(8,128)S(1)} %get-tuple-element.5.carried, s32[32,8192]{1,0:T(8,128)S(1)} %copy-done), custom_call_target="tpu_custom_call" | custom-call | tf_op jit(solution)/shard_map/finish/pallas_call | solution.py:408
Async XLA Ops:
  0.6 37.2 %copy-start = (s32[32,8192]{1,0:T(8,128)S(1)}, s32[32,8192]{1,0:T(8,128)}, u32[]{:S(2)}) copy-start(s32[32,8192]{1,0:T(8,128)} %ids.3) | copy-start | bytes 3145732

commit v9 on v8

--- a/solution.py
+++ b/solution.py
@@ -177,10 +177,6 @@
     slots = leaf_slots(TILE)
     trees = pl.ds(pl.multiple_of(slot // 2 * TREES_AT_ONCE, TREES_AT_ONCE), TREES_AT_ONCE)
 
-    @pl.when(slot % 2 == 0)
-    def _():
-        acc[...] = jnp.zeros_like(acc)
-
     @pl.loop(0, rows, step=TILE * UNROLL)
     def _(first):
         total = None
@@ -191,7 +187,15 @@
                 matches, stacked[:, cols], (((1,), (1,)), ((), ())), preferred_element_type=F32
             )
             total = part if total is None else total + part
-        acc[...] += total
+        fresh = jnp.logical_and(slot % 2 == 0, first == 0)
+
+        @pl.when(fresh)
+        def _():
+            acc[...] = total
+
+        @pl.when(jnp.logical_not(fresh))
+        def _():
+            acc[...] += total
 
 
 def keep_sums(c, acc, sums):

time: 41 us -> 41.2 us (level)
  no operation moved by 1% of the time
where the time goes in v9:
time: 41.2 us; the launch traced here: 41.1 us
  Pallas kernels  40.4 us (98%)
  between operations  0.65 us (2%)
    pallas_call x1, Pallas kernels, grow(): pl.pallas_call(grow_kernel, out_shape=(jax.ShapeDtypeStruct(predict.shape...  37.4 us
    pallas_call x1, Pallas kernels, finish(): pl.pallas_call(finish_kernel, out_shape=(jax.ShapeDtypeStruct(carried.sha...  3.04 us

profile of v9, /device:TPU:1, one launch (start us, length us, event | category | flops | bytes accessed | tf_op | source)
XLA Modules:
  0.0 41.1 jit_solution(15673333111173157977)
XLA Ops:
  0.6 0.0 copy-start
  0.6 37.4 %grow.1 = (f32[100,8192]{1,0:T(8,128)S(1)}, f32[2048,128]{1,0:T(8,128)S(1)}) custom-call(f32[100,8192]{1,0:T(8,128)} %predict.1, s32[1,8192]{1,0:T(1,128)} %bitcast.1, s32[32,8192]{1,0:T(8,128)} %ids.3), custom_call_target="tpu_custom_call" | custom-call | tf_op jit(solution)/shard_map/grow/pallas_call | solution.py:356
  38.0 0.0 copy-done
  38.0 3.0 %finish.1 = (f32[100,8192]{1,0:T(8,128)}, f32[100,512]{1,0:T(8,128)}) custom-call(f32[2048,128]{1,0:T(8,128)S(1)} %get-tuple-element.4.values, f32[100,8192]{1,0:T(8,128)S(1)} %get-tuple-element.5.carried, s32[32,8192]{1,0:T(8,128)S(1)} %copy-done), custom_call_target="tpu_custom_call" | custom-call | tf_op jit(solution)/shard_map/finish/pallas_call | solution.py:412
Async XLA Ops:
  0.6 37.4 %copy-start = (s32[32,8192]{1,0:T(8,128)S(1)}, s32[32,8192]{1,0:T(8,128)}, u32[]{:S(2)}) copy-start(s32[32,8192]{1,0:T(8,128)} %ids.3) | copy-start | bytes 3145732
